TPU v7x, 32 devices: a whole 2x2x4 slice. The times are simulated.
32 devices in a mesh: first: 8 (over z, core), second: 4 (over y, x).
Axes of the slice: x: 2, y: 2, z: 4, core: 2. Of those that a mesh axis runs over, the one named last changes fastest.
Arguments:
- pair_rows: bfloat16 [96, 96, 128], P('first', 'second'), may hold values from -6 to 6
- in_gain: float32 [128], replicated, may hold values from 0.25 to 1.75
- left_weight: bfloat16 [128, 128], replicated, may hold values from -0.5 to 0.5
- right_weight: bfloat16 [128, 128], replicated, may hold values from -0.5 to 0.5
- mid_gain: float32 [128], replicated, may hold values from 0.25 to 1.75
- out_weight: bfloat16 [128, 128], replicated, may hold values from -0.5 to 0.5
- out_gate: bfloat16 [128, 128], replicated, may hold values from -0.5 to 0.5
Outputs:
- triangle_out: bfloat16 [96, 96, 128], P('first', 'second')
All inputs are finite; a program needn't handle non-finite values.
Results may differ from a plain program's by a relative error of at most 0.012.
Values may be sent and summed in bfloat16 or wider, within the bound.
A program may use at most 64 MiB of HBM per device.

v0:
```python
import functools

import jax
import jax.numpy as jnp
from jax import lax
from jax.experimental import pallas as pl
from jax.experimental.pallas import tpu as pltpu
from jax.sharding import PartitionSpec as P

MESH = pl.DeviceIdType.MESH


def norm_channels(values, channel_gain):
    centred = values - jnp.mean(values, axis=-1, keepdims=True)
    return (
        centred
        * lax.rsqrt(jnp.mean(centred * centred, axis=-1, keepdims=True) + 1e-05)
        * channel_gain
    )


def flip(index, bits, count):
    out, weight = 0, 1
    while weight < count:
        out = out + weight * lax.rem(lax.div(index, weight) + (bits // weight) % 2, 2)
        weight *= 2
    return out


def dot(a, b):
    return jnp.dot(a, b, preferred_element_type=jnp.float32)


def triangle_kernel(
    rows, cols, planes, lines,
    x_ref, in_gain_ref, left_w_ref, right_w_ref, mid_gain_ref, out_w_ref, gate_w_ref,
    out_ref,
    split, lsend, lrecv, rsend, rrecv, left32, right32, own, psend, precv, gate,
    lsend_sem, lrecv_sem, rsend_sem, rrecv_sem, psend_sem, precv_sem,
):
    first, second = lax.axis_index("first"), lax.axis_index("second")
    z, core = lax.div(first, 2), lax.rem(first, 2)
    pairs = rows * cols
    half = cols // 2

    def device(z_at, core_at, second_at):
        return {"first": 2 * z_at + core_at, "second": second_at}

    barrier = pltpu.get_barrier_semaphore()
    peers = 0
    for t in range(lines):
        for rel in range(2):
            if t or rel:
                to = device(z, lax.rem(core + rel, 2), flip(second, t, lines))
                pl.semaphore_signal(barrier, inc=1, device_id=to, device_id_type=MESH)
                peers += 1
    for dz in range(1, planes):
        to = device(lax.rem(z + dz, planes), core, second)
        pl.semaphore_signal(barrier, inc=1, device_id=to, device_id_type=MESH)
        peers += 1

    ready = norm_channels(x_ref[...].astype(jnp.float32), in_gain_ref[...]).astype(jnp.bfloat16)
    left = dot(ready, left_w_ref[...])
    for k in range(rows):
        for h in range(2):
            at = k * cols + h * half
            split[h, k * half : (k + 1) * half, :] = left[at : at + half, :]
    for h in range(2):
        lsend[h] = split[h].astype(jnp.bfloat16)
    right = dot(ready, right_w_ref[...]).astype(jnp.bfloat16)
    rsend[...] = right

    pl.semaphore_wait(barrier, peers)

    left_copies = {}
    for t in range(lines - 1, -1, -1):
        for rel in range(2):
            if t or rel:
                to_core = lax.rem(core + rel, 2)
                copy = pltpu.make_async_remote_copy(
                    src_ref=lsend.at[to_core],
                    dst_ref=lrecv.at[t, rel],
                    send_sem=lsend_sem.at[t, rel],
                    recv_sem=lrecv_sem.at[t, rel],
                    device_id=device(z, to_core, flip(second, t, lines)),
                    device_id_type=MESH,
                )
                copy.start()
                left_copies[t, rel] = copy
    right_copy = pltpu.make_async_remote_copy(
        src_ref=rsend,
        dst_ref=rrecv,
        send_sem=rsend_sem,
        recv_sem=rrecv_sem,
        device_id=device(z, 1 - core, second),
        device_id_type=MESH,
    )
    right_copy.start()

    gate[...] = jax.nn.sigmoid(dot(ready, gate_w_ref[...]))
    right32[0] = right.astype(jnp.float32)
    right_copy.wait_recv()
    right32[1] = rrecv[...].astype(jnp.float32)

    part_copies = []
    for t in range(lines):
        for rel in range(2):
            if t or rel:
                left_copies[t, rel].wait_recv()
                left32[rel] = lrecv[t, rel].astype(jnp.float32)
            else:
                left32[rel] = lsend[core].astype(jnp.float32)

        sums = tuple(jnp.zeros((cols, x_ref.shape[1]), jnp.float32) for _ in range(half))
        for rel in range(2):

            def body(k, sums):
                r = right32[rel, pl.ds(pl.multiple_of(k * cols, 8), cols), :]
                return tuple(
                    total + left32[rel, pl.ds(k * half + i, 1), :] * r
                    for i, total in enumerate(sums)
                )

            sums = lax.fori_loop(0, rows, body, sums)

        z_to = flip(second, t, lines)
        is_own = z_to == z

        @pl.when(is_own)
        def _():
            for i, total in enumerate(sums):
                own[i * cols : (i + 1) * cols, :] = total

        for i in range(0, half, 2):
            two = jnp.concatenate([sums[i], sums[i + 1]], axis=0)
            psend[t, i * cols : (i + 2) * cols, :] = two.astype(jnp.bfloat16)
        slot = lax.rem(z - z_to + 2 * planes - 1, planes)
        copy = pltpu.make_async_remote_copy(
            src_ref=psend.at[t],
            dst_ref=precv.at[slot],
            send_sem=psend_sem.at[t],
            recv_sem=precv_sem.at[slot],
            device_id=device(z_to, core, second),
            device_id_type=MESH,
        )
        part_copies.append((is_own, copy))

        @pl.when(jnp.logical_not(is_own))
        def _():
            copy.start()

    total = own[...]
    for slot in range(planes - 1):
        pltpu.make_async_remote_copy(
            src_ref=psend.at[0],
            dst_ref=precv.at[slot],
            send_sem=psend_sem.at[0],
            recv_sem=precv_sem.at[slot],
            device_id=device(lax.rem(z + 1, planes), core, second),
            device_id_type=MESH,
        ).wait_recv()
        total = total + precv[slot].astype(jnp.float32)
    count = rows * 2 * planes
    mixed = (total * count ** (-0.5)).astype(jnp.bfloat16)
    scaled = norm_channels(mixed.astype(jnp.float32), mid_gain_ref[...]).astype(jnp.bfloat16)
    out_ref[...] = (dot(scaled, out_w_ref[...]) * gate[...]).astype(jnp.bfloat16)

    for copy in left_copies.values():
        copy.wait_send()
    right_copy.wait_send()
    for is_own, copy in part_copies:

        @pl.when(jnp.logical_not(is_own))
        def _():
            copy.wait_send()


def triangle(planes, lines, pair_rows, in_gain, left_weight, right_weight, mid_gain, out_weight, out_gate):
    rows, cols, width = pair_rows.shape
    mix = left_weight.shape[1]
    pairs, half = rows * cols, cols // 2
    vmem = pl.BlockSpec(memory_space=pltpu.VMEM)
    bf16, f32 = jnp.bfloat16, jnp.float32
    out = pl.pallas_call(
        functools.partial(triangle_kernel, rows, cols, planes, lines),
        out_shape=jax.ShapeDtypeStruct((pairs, width), bf16),
        in_specs=[vmem] * 7,
        out_specs=vmem,
        scratch_shapes=[
            pltpu.VMEM((2, rows * half, mix), f32),
            pltpu.VMEM((2, rows * half, mix), bf16),
            pltpu.VMEM((lines, 2, rows * half, mix), bf16),
            pltpu.VMEM((pairs, mix), bf16),
            pltpu.VMEM((pairs, mix), bf16),
            pltpu.VMEM((2, rows * half, mix), f32),
            pltpu.VMEM((2, pairs, mix), f32),
            pltpu.VMEM((half * cols, mix), f32),
            pltpu.VMEM((lines, half * cols, mix), bf16),
            pltpu.VMEM((planes - 1, half * cols, mix), bf16),
            pltpu.VMEM((pairs, width), f32),
            pltpu.SemaphoreType.DMA((lines, 2)),
            pltpu.SemaphoreType.DMA((lines, 2)),
            pltpu.SemaphoreType.DMA,
            pltpu.SemaphoreType.DMA,
            pltpu.SemaphoreType.DMA((lines,)),
            pltpu.SemaphoreType.DMA((planes - 1,)),
        ],
        compiler_params=pltpu.CompilerParams(collective_id=0, has_side_effects=True),
    )(
        pair_rows.reshape(pairs, width), in_gain.reshape(1, width), left_weight, right_weight,
        mid_gain.reshape(1, mix), out_weight, out_gate,
    )
    return out.reshape(rows, cols, width)


def shards(pair_rows, in_gain, left_weight, right_weight, mid_gain, out_weight, out_gate):
    ready = norm_channels(pair_rows.astype(jnp.float32), in_gain).astype(jnp.bfloat16)
    ready = lax.optimization_barrier(ready)
    left = jnp.einsum("ijc,cd->ijd", ready, left_weight, preferred_element_type=jnp.float32)
    right = jnp.einsum("ijc,cd->ijd", ready, right_weight, preferred_element_type=jnp.float32)
    left, right = left.astype(jnp.bfloat16), right.astype(jnp.bfloat16)
    count = pair_rows.shape[0] * lax.axis_size("first")
    left_lines, right_lines = (
        lax.all_to_all(left, "first", split_axis=2, concat_axis=0, tiled=True),
        lax.all_to_all(right, "first", split_axis=2, concat_axis=0, tiled=True),
    )
    strip = jnp.einsum(
        "kid,kjd->ijd",
        lax.all_gather(left_lines, "second", axis=1, tiled=True),
        right_lines,
        preferred_element_type=jnp.float32,
    )
    strip = (strip * count ** (-0.5)).astype(jnp.bfloat16)
    mixed = lax.all_to_all(strip, "first", split_axis=0, concat_axis=2, tiled=True)
    scaled = norm_channels(mixed.astype(jnp.float32), mid_gain).astype(jnp.bfloat16)
    scaled = lax.optimization_barrier(scaled)
    gate = jax.nn.sigmoid(
        jnp.einsum("ijc,cd->ijd", ready, out_gate, preferred_element_type=jnp.float32)
    )
    return (
        jnp.einsum("ijd,dc->ijc", scaled, out_weight, preferred_element_type=jnp.float32) * gate
    ).astype(jnp.bfloat16)


def solution(mesh):
    in_specs = (P("first", "second", None), P(), P(), P(), P(), P(), P())
    out_specs = P("first", "second", None)
    planes, lines = mesh.shape["first"] // 2, mesh.shape["second"]
    if mesh.shape["first"] == 2 * lines and lines & (lines - 1) == 0:
        body = functools.partial(triangle, planes, lines)
    else:
        body = shards
    return jax.shard_map(body, mesh=mesh, in_specs=in_specs, out_specs=out_specs, check_vma=False)
```

profile of v0, /device:TPU:6, one launch (start us, length us, event | category | flops | bytes accessed | tf_op | source)
XLA Modules:
  0.0 20.4 jit_solution(268367610929308448)
XLA Ops:
  0.0 18.9 %shard_map.73 = bf16[288,128]{1,0:T(8,128)(2,1)} custom-call(bf16[288,128]{1,0:T(8,128)(2,1)} %bitcast.5, f32[1,128]{1,0:T(1,128)} %bitcast.6, bf16[128,128]{1,0:T(8,128)(2,1)} %left_w_ref.1, bf16[128,128]{1,0:T(8,128)(2,1)} %right_w_ref.1, f32[1,128]{1,0:T(1,128)} %bitcast.7, bf16[128,128]{1,0:T(8,128)(2,1)} %out_w_ref.1, bf16[128,128]{1,0:T(8,128)(2,1)} %gate_w_ref.1), custom_call_target="tpu_custom_call" | custom-call | tf_op jit(solution)/shard_map/pallas_call | solution.py:184
  18.9 1.5 %copy.9 = bf16[12,24,128]{2,1,0:T(8,128)(2,1)} copy(bf16[12,24,128]{2,1,0:T(8,128)(2,1)} %bitcast.4) | data formatting | bytes 147456
where the time goes:
time: 20.6 us; the launch traced here: 20.4 us
  Pallas kernels  18.9 us (92%)
  local copies, waits for them, and re-layouts  1.52 us (7%)
    pallas_call x1, Pallas kernels, triangle(): pl.pallas_call(functools.partial(triangle_kernel, rows, cols, planes, lin...  18.9 us
    unnamed x1, local copies, waits for them, and re-layouts  1.52 us

commit v1 on v0

--- a/solution.py
+++ b/solution.py
@@ -183,7 +183,7 @@
     bf16, f32 = jnp.bfloat16, jnp.float32
     out = pl.pallas_call(
         functools.partial(triangle_kernel, rows, cols, planes, lines),
-        out_shape=jax.ShapeDtypeStruct((pairs, width), bf16),
+        out_shape=pltpu.VMEM((pairs, width), bf16),
         in_specs=[vmem] * 7,
         out_specs=vmem,
         scratch_shapes=[

time: 20.6 us -> 19 us (0.922)
  local copies, waits for them, and re-layouts: 1.52 us -> 0.64 us
  Pallas kernels: 18.9 us -> 18.2 us
    unnamed x1, local copies, waits for them, and re-layouts: 1.52 us -> 0.64 us
    pallas_call x1, Pallas kernels: 18.9 us -> 18.2 us  [triangle(): pl.pallas_call(functools.partial(triangle_kernel, rows, cols, planes, lin...]
where the time goes in v1:
time: 19 us; the launch traced here: 18.9 us
  Pallas kernels  18.2 us (96%)
  local copies, waits for them, and re-layouts  0.64 us (3%)
    pallas_call x1, Pallas kernels, triangle(): pl.pallas_call(functools.partial(triangle_kernel, rows, cols, planes, lin...  18.2 us
    unnamed x1, local copies, waits for them, and re-layouts  0.64 us

profile of v1, /device:TPU:6, one launch (start us, length us, event | category | flops | bytes accessed | tf_op | source)
XLA Modules:
  0.0 18.9 jit_solution(17849798080422224417)
XLA Ops:
  0.0 18.2 %shard_map.73 = bf16[288,128]{1,0:T(8,128)(2,1)S(1)} custom-call(bf16[288,128]{1,0:T(8,128)(2,1)} %bitcast.5, f32[1,128]{1,0:T(1,128)} %bitcast.6, bf16[128,128]{1,0:T(8,128)(2,1)} %left_w_ref.1, bf16[128,128]{1,0:T(8,128)(2,1)} %right_w_ref.1, f32[1,128]{1,0:T(1,128)} %bitcast.7, bf16[128,128]{1,0:T(8,128)(2,1)} %out_w_ref.1, bf16[128,128]{1,0:T(8,128)(2,1)} %gate_w_ref.1), custom_call_target="tpu_custom_call" | custom-call | tf_op jit(solution)/shard_map/pallas_call | solution.py:184
  18.2 0.6 %copy.9 = bf16[12,24,128]{2,1,0:T(8,128)(2,1)} copy(bf16[12,24,128]{2,1,0:T(8,128)(2,1)S(1)} %bitcast.4) | data formatting | bytes 147456

commit v2 on v1

v2 whole, which is shorter than its diff:
```python
import functools

import jax
import jax.numpy as jnp
from jax import lax
from jax.experimental import pallas as pl
from jax.experimental.pallas import tpu as pltpu
from jax.sharding import PartitionSpec as P

MESH = pl.DeviceIdType.MESH


def norm_channels(values, channel_gain):
    centred = values - jnp.mean(values, axis=-1, keepdims=True)
    return (
        centred
        * lax.rsqrt(jnp.mean(centred * centred, axis=-1, keepdims=True) + 1e-05)
        * channel_gain
    )


def flip(index, bits, count):
    out, weight = 0, 1
    while weight < count:
        out = out + weight * lax.rem(lax.div(index, weight) + (bits // weight) % 2, 2)
        weight *= 2
    return out


def dot(a, b):
    return jnp.dot(a, b, preferred_element_type=jnp.float32)


CHUNK = 4


def flip_low(index):
    return index + 1 - 2 * lax.rem(index, 2)


def triangle_kernel(
    rows, cols, planes, lines,
    x_hbm, in_gain_hbm, left_w_hbm, right_w_hbm, mid_gain_hbm, out_w_hbm, gate_w_hbm,
    out_ref,
    x_ref, in_gain_ref, left_w_ref, right_w_ref, mid_gain_ref, out_w_ref, gate_w_ref,
    lsend, lrecv, rsend, left32, right32, psend, part32, inbox, gate,
    in_sem, lsend_sem, lrecv_sem, rsend_sem, rrecv_sem, psend_sem, inbox_sem, go_sem,
):
    first, second = lax.axis_index("first"), lax.axis_index("second")
    z, core = lax.div(first, 2), lax.rem(first, 2)
    pairs = rows * cols
    chunks = cols // CHUNK
    per_core = chunks // 2
    size = CHUNK * cols
    half = planes // 2
    upper, side = lax.div(z, half), lax.div(second, half)
    near_z = flip_low(z)
    inner = lax.rem(z, 2) != upper

    def device(z_at, core_at, second_at):
        return {"first": 2 * z_at + core_at, "second": second_at}

    scope = jax.named_scope
    barrier = pltpu.get_barrier_semaphore()

    def greet(to):
        pl.semaphore_signal(barrier, inc=1, device_id=to, device_id_type=MESH)

    with scope("sig"):
        for t in range(lines):
            for rel in range(2):
                if t or rel:
                    greet(device(z, lax.rem(core + rel, 2), flip(second, t, lines)))
        for dz in (1, 2):
            for c in range(2):
                greet(device(flip(z, dz, planes), c, second))

        @pl.when(inner)
        def _():
            for c in range(2):
                greet(device(flip(z, 3, planes), c, second))

    loads = [
        pltpu.make_async_copy(src, dst, in_sem.at[n])
        for n, (src, dst) in enumerate((
            (x_hbm, x_ref), (in_gain_hbm, in_gain_ref), (left_w_hbm, left_w_ref), (right_w_hbm, right_w_ref),
            (gate_w_hbm, gate_w_ref), (mid_gain_hbm, mid_gain_ref), (out_w_hbm, out_w_ref),
        ))
    ]
    for load in loads:
        load.start()
    with scope("load"):
        for load in loads[:3]:
            load.wait()

    with scope("left"):
        ready = norm_channels(x_ref[...].astype(jnp.float32), in_gain_ref[...]).astype(jnp.bfloat16)
        left = dot(ready, left_w_ref[...]).astype(jnp.bfloat16)
        lsend[...] = left
        lrecv[0, core] = left

    with scope("bar"):
        pl.semaphore_wait(barrier, 2 * lines - 1 + 4 + 2 * inner.astype(jnp.int32))

    target = lax.rem(side + upper, 2)

    def left_copy(t):
        return pltpu.make_async_remote_copy(
            src_ref=lsend,
            dst_ref=lrecv.at[t, core],
            send_sem=lsend_sem.at[t],
            recv_sem=lrecv_sem.at[t, core],
            device_id=device(z, target, flip(second, t, lines)),
            device_id_type=MESH,
        )

    for t in (2, 1, 3):
        left_copy(t).start()

    @pl.when(target != core)
    def _():
        left_copy(0).start()

    with scope("right"):
        loads[3].wait()
        right = dot(ready, right_w_ref[...]).astype(jnp.bfloat16)
        rsend[core] = right
    right_copy = pltpu.make_async_remote_copy(
        src_ref=rsend.at[core],
        dst_ref=rsend.at[core],
        send_sem=rsend_sem,
        recv_sem=rrecv_sem,
        device_id=device(z, 1 - core, second),
        device_id_type=MESH,
    )
    right_copy.start()
    with scope("gate"):
        loads[4].wait()
        gate[...] = jax.nn.sigmoid(dot(ready, gate_w_ref[...]))
        loads[5].wait()
        loads[6].wait()
    with scope("rwait"):
        right_copy.wait_recv()
    with scope("r32"):
        for q in range(2):
            right32[q * pairs : (q + 1) * pairs, :] = rsend[q].astype(jnp.float32)

    target_side = jnp.where(core == 1, 1 - upper, upper)
    t_high = lax.rem(side + target_side, 2)

    def block_plane(u):
        return half * target_side + lax.rem(lax.rem(second, 2) + u, 2)

    def send(u, c, slot, to):
        return pltpu.make_async_remote_copy(
            src_ref=psend.at[u, c],
            dst_ref=inbox.at[slot],
            send_sem=psend_sem.at[u, c],
            recv_sem=inbox_sem.at[slot],
            device_id=to,
            device_id_type=MESH,
        )

    near_at, cross_at, own_at = 2 * chunks, 2 * chunks + per_core, 2 * chunks + 2 * per_core
    crossing = core == 1
    outer = jnp.logical_not(inner)
    t_near = 2 * lax.rem(side + upper, 2) + lax.rem(lax.rem(second, 2) + lax.rem(near_z, 2), 2)
    held_back = jnp.logical_and(outer, t_near != 0)

    for u in range(2):
        t_at = half * t_high + u
        plane = block_plane(u)
        is_own = plane == z
        for q in range(2):
            mine = jnp.logical_and(t_at == 0, core == q)

            with scope(f"wl{u}{q}"):

                @pl.when(jnp.logical_not(mine))
                def _():
                    pltpu.make_async_remote_copy(
                        src_ref=lsend,
                        dst_ref=lrecv.at[t_at, q],
                        send_sem=lsend_sem.at[0],
                        recv_sem=lrecv_sem.at[t_at, q],
                        device_id=device(z, 1 - core, second),
                        device_id_type=MESH,
                    ).wait_recv()

            left32[q * pairs : (q + 1) * pairs, :] = lrecv[t_at, q].astype(jnp.float32)

        with scope(f"block{u}"):
            for c in range(chunks):

                def body(k, sums):
                    r = right32[pl.ds(pl.multiple_of(k * cols, 8), cols), :]
                    return tuple(
                        total + left32[pl.ds(k * cols + c * CHUNK + i, 1), :] * r
                        for i, total in enumerate(sums)
                    )

                sums = lax.fori_loop(
                    0, 2 * rows, body,
                    tuple(jnp.zeros((cols, x_ref.shape[1]), jnp.float32) for _ in range(CHUNK)),
                    unroll=8,
                )
                total = jnp.concatenate(sums, axis=0)
                part32[u, c] = total
                psend[u, c] = total.astype(jnp.bfloat16)
                to_core = c // per_core

                @pl.when(jnp.logical_and(crossing, outer))
                def _():
                    send(u, c, u * chunks + c, device(near_z, 1, second)).start()

                if to_core == 1:

                    @pl.when(jnp.logical_and(jnp.logical_not(crossing), is_own))
                    def _():
                        send(u, c, own_at + c % per_core, device(z, 1, second)).start()

                @pl.when(
                    jnp.logical_not(jnp.logical_or(crossing, jnp.logical_or(is_own, held_back)))
                )
                def _():
                    send(u, c, near_at + c % per_core, device(near_z, to_core, second)).start()

    def each(what):
        for u in range(2):
            for c in range(chunks):
                what(u, c, send(u, c, near_at + c % per_core, device(near_z, c // per_core, second)))

    with scope("relay"):

        @pl.when(jnp.logical_and(crossing, inner))
        def _():
            for u in range(2):
                for c in range(chunks):
                    send(u, c, u * chunks + c, device(near_z, 1, second)).wait_recv()
                    total = part32[u, c] + inbox[u * chunks + c].astype(jnp.float32)
                    psend[u, c] = total.astype(jnp.bfloat16)
                    send(
                        u, c, cross_at + c % per_core, device(block_plane(u), c // per_core, second)
                    ).start()

    with scope("held"):

        @pl.when(held_back)
        def _():
            @pl.when(crossing)
            def _():
                each(lambda u, c, copy: copy.wait_send())
                pl.semaphore_signal(go_sem, inc=1, device_id=device(z, 0, second), device_id_type=MESH)

            @pl.when(jnp.logical_not(crossing))
            def _():
                pl.semaphore_wait(go_sem, 1)
                for u in range(2):

                    @pl.when(block_plane(u) != z)
                    def _():
                        for c in range(chunks):
                            send(
                                u, c, near_at + c % per_core, device(near_z, c // per_core, second)
                            ).start()

    own_u = lax.rem(lax.rem(second, 2) + lax.rem(z, 2), 2)
    count = rows * 2 * planes
    for c in range(per_core):
        with scope(f"own{c}"):

            @pl.when(crossing)
            def _():
                send(0, c, own_at + c, device(z, 0, second)).wait_recv()
                part32[0, c] = inbox[own_at + c].astype(jnp.float32)

            at_own = jnp.where(crossing, 0, own_u)
        with scope(f"near{c}"):
            send(0, c, near_at + c, device(near_z, 0, second)).wait_recv()
        with scope(f"cross{c}"):
            send(0, c, cross_at + c, device(near_z, 0, second)).wait_recv()
        with scope(f"final{c}"):
            total = (
                part32[at_own, c]
                + inbox[near_at + c].astype(jnp.float32)
                + inbox[cross_at + c].astype(jnp.float32)
            )
            mixed = (total * count ** (-0.5)).astype(jnp.bfloat16)
            scaled = norm_channels(mixed.astype(jnp.float32), mid_gain_ref[...]).astype(jnp.bfloat16)
            at = slice(c * size, (c + 1) * size)
            out_ref[at, :] = (dot(scaled, out_w_ref[...]) * gate[at, :]).astype(jnp.bfloat16)

    with scope("drain"):
        for t in (1, 2, 3):
            left_copy(t).wait_send()

        @pl.when(target != core)
        def _():
            left_copy(0).wait_send()

        right_copy.wait_send()

        @pl.when(crossing)
        def _():
            @pl.when(jnp.logical_not(held_back))
            def _():
                each(lambda u, c, copy: copy.wait_send())

        @pl.when(jnp.logical_not(crossing))
        def _():
            for u in range(2):

                @pl.when(block_plane(u) != z)
                def _():
                    for c in range(per_core):
                        send(u, c, near_at + c, device(near_z, 0, second)).wait_send()

                for c in range(per_core, chunks):
                    send(u, c, near_at + c - per_core, device(near_z, 1, second)).wait_send()


def triangle(planes, lines, pair_rows, in_gain, left_weight, right_weight, mid_gain, out_weight, out_gate):
    rows, cols, width = pair_rows.shape
    mix = left_weight.shape[1]
    pairs, chunks, size = rows * cols, cols // CHUNK, CHUNK * cols
    slots = 2 * chunks + 3 * (chunks // 2)
    anywhere = pl.BlockSpec(memory_space=pl.ANY)
    bf16, f32 = jnp.bfloat16, jnp.float32
    out = pl.pallas_call(
        functools.partial(triangle_kernel, rows, cols, planes, lines),
        out_shape=pltpu.VMEM((pairs, width), bf16),
        in_specs=[anywhere] * 7,
        out_specs=pl.BlockSpec(memory_space=pltpu.VMEM),
        scratch_shapes=[
            pltpu.VMEM((pairs, width), bf16),
            pltpu.VMEM((1, width), f32),
            pltpu.VMEM((width, mix), bf16),
            pltpu.VMEM((width, mix), bf16),
            pltpu.VMEM((1, mix), f32),
            pltpu.VMEM((mix, width), bf16),
            pltpu.VMEM((width, width), bf16),
            pltpu.VMEM((pairs, mix), bf16),
            pltpu.VMEM((lines, 2, pairs, mix), bf16),
            pltpu.VMEM((2, pairs, mix), bf16),
            pltpu.VMEM((2 * pairs, mix), f32),
            pltpu.VMEM((2 * pairs, mix), f32),
            pltpu.VMEM((2, chunks, size, mix), bf16),
            pltpu.VMEM((2, chunks, size, mix), f32),
            pltpu.VMEM((slots, size, mix), bf16),
            pltpu.VMEM((pairs, width), f32),
            pltpu.SemaphoreType.DMA((7,)),
            pltpu.SemaphoreType.DMA((lines,)),
            pltpu.SemaphoreType.DMA((lines, 2)),
            pltpu.SemaphoreType.DMA,
            pltpu.SemaphoreType.DMA,
            pltpu.SemaphoreType.DMA((2, chunks)),
            pltpu.SemaphoreType.DMA((slots,)),
            pltpu.SemaphoreType.REGULAR,
        ],
        compiler_params=pltpu.CompilerParams(collective_id=0, has_side_effects=True),
    )(
        pair_rows.reshape(pairs, width), in_gain.reshape(1, width), left_weight, right_weight,
        mid_gain.reshape(1, mix), out_weight, out_gate,
    )
    return out.reshape(rows, cols, width)


def shards(pair_rows, in_gain, left_weight, right_weight, mid_gain, out_weight, out_gate):
    ready = norm_channels(pair_rows.astype(jnp.float32), in_gain).astype(jnp.bfloat16)
    ready = lax.optimization_barrier(ready)
    left = jnp.einsum("ijc,cd->ijd", ready, left_weight, preferred_element_type=jnp.float32)
    right = jnp.einsum("ijc,cd->ijd", ready, right_weight, preferred_element_type=jnp.float32)
    left, right = left.astype(jnp.bfloat16), right.astype(jnp.bfloat16)
    count = pair_rows.shape[0] * lax.axis_size("first")
    left_lines, right_lines = (
        lax.all_to_all(left, "first", split_axis=2, concat_axis=0, tiled=True),
        lax.all_to_all(right, "first", split_axis=2, concat_axis=0, tiled=True),
    )
    strip = jnp.einsum(
        "kid,kjd->ijd",
        lax.all_gather(left_lines, "second", axis=1, tiled=True),
        right_lines,
        preferred_element_type=jnp.float32,
    )
    strip = (strip * count ** (-0.5)).astype(jnp.bfloat16)
    mixed = lax.all_to_all(strip, "first", split_axis=0, concat_axis=2, tiled=True)
    scaled = norm_channels(mixed.astype(jnp.float32), mid_gain).astype(jnp.bfloat16)
    scaled = lax.optimization_barrier(scaled)
    gate = jax.nn.sigmoid(
        jnp.einsum("ijc,cd->ijd", ready, out_gate, preferred_element_type=jnp.float32)
    )
    return (
        jnp.einsum("ijd,dc->ijc", scaled, out_weight, preferred_element_type=jnp.float32) * gate
    ).astype(jnp.bfloat16)


def solution(mesh):
    in_specs = (P("first", "second", None), P(), P(), P(), P(), P(), P())
    out_specs = P("first", "second", None)
    planes, lines = mesh.shape["first"] // 2, mesh.shape["second"]
    if planes == lines == 4:
        body = functools.partial(triangle, planes, lines)
    else:
        body = shards
    return jax.shard_map(body, mesh=mesh, in_specs=in_specs, out_specs=out_specs, check_vma=False)
```

time: 19 us -> 16.6 us (0.87)
  the two profiles are of different devices: /device:TPU:6 before, /device:TPU:0 now
where the time goes in v2:
time: 16.6 us; the launch traced here: 16.5 us
  Pallas kernels  15.8 us (95%)
  local copies, waits for them, and re-layouts  0.64 us (4%)
    pallas_call x1, Pallas kernels, triangle(): pl.pallas_call(functools.partial(triangle_kernel, rows, cols, planes, lin...  15.8 us
    unnamed x1, local copies, waits for them, and re-layouts  0.64 us

profile of v2, /device:TPU:0, one launch (start us, length us, event | category | flops | bytes accessed | tf_op | source)
XLA Modules:
  0.0 16.5 jit_solution(15986527347622940830)
XLA Ops:
  0.0 15.8 %shard_map.73 = bf16[288,128]{1,0:T(8,128)(2,1)S(1)} custom-call(bf16[288,128]{1,0:T(8,128)(2,1)} %bitcast.5, f32[1,128]{1,0:T(1,128)} %bitcast.6, bf16[128,128]{1,0:T(8,128)(2,1)} %left_w_hbm.1, bf16[128,128]{1,0:T(8,128)(2,1)} %right_w_hbm.1, f32[1,128]{1,0:T(1,128)} %bitcast.7, bf16[128,128]{1,0:T(8,128)(2,1)} %out_w_hbm.1, bf16[128,128]{1,0:T(8,128)(2,1)} %gate_w_hbm.1), custom_call_target="tpu_custom_call" | custom-call | tf_op jit(solution)/shard_map/pallas_call | solution.py:329
  15.9 0.6 %copy.9 = bf16[12,24,128]{2,1,0:T(8,128)(2,1)} copy(bf16[12,24,128]{2,1,0:T(8,128)(2,1)S(1)} %bitcast.4) | data formatting | bytes 147456

commit v3 on v2

v3 whole, which is shorter than its diff:
```python
import functools

import jax
import jax.numpy as jnp
from jax import lax
from jax.experimental import pallas as pl
from jax.experimental.pallas import tpu as pltpu
from jax.sharding import PartitionSpec as P

MESH = pl.DeviceIdType.MESH


def norm_channels(values, channel_gain):
    centred = values - jnp.mean(values, axis=-1, keepdims=True)
    return (
        centred
        * lax.rsqrt(jnp.mean(centred * centred, axis=-1, keepdims=True) + 1e-05)
        * channel_gain
    )


def dot(a, b):
    return jnp.dot(a, b, preferred_element_type=jnp.float32)


PIECE = 8
CHUNK = 4


def other(index):
    return index + 1 - 2 * lax.rem(index, 2)


def triangle_kernel(
    rows, cols, planes, lines,
    x_hbm, in_gain_hbm, left_w_hbm, right_w_hbm, mid_gain_hbm, out_w_hbm, gate_w_hbm,
    out_ref,
    x_ref, in_gain_ref, left_w_ref, right_w_ref, mid_gain_ref, out_w_ref, gate_w_ref,
    lsend, lrecv, rboth, left32, right32, psend, part32, inbox, gate,
    in_sem, lsend_sem, lrecv_sem, rsend_sem, rrecv_sem, psend_sem, inbox_sem, go_sem,
):
    first, second = lax.axis_index("first"), lax.axis_index("second")
    z, core = lax.div(first, 2), lax.rem(first, 2)
    pieces, chunks = cols // PIECE, cols // CHUNK
    per_piece, per_core = PIECE // CHUNK, chunks // 2
    lump, size = rows * PIECE, CHUNK * cols
    half = planes // 2
    upper, side, parity = lax.div(z, half), lax.div(second, half), lax.rem(second, 2)
    near_z = other(z)
    inner = lax.rem(z, 2) != upper
    outer = jnp.logical_not(inner)
    crossing = core == 1
    level = core == 0
    target_side = jnp.where(crossing, 1 - upper, upper)
    planes_of = [half * target_side + lax.rem(parity + u, 2) for u in range(2)]
    from_own = target_side == side
    is_own = [jnp.logical_and(level, planes_of[u] == z) for u in range(2)]
    is_near = [jnp.logical_and(level, planes_of[u] != z) for u in range(2)]
    x_second, y_second = other(second), lax.rem(second + half, lines)
    xy_second = other(y_second)
    cross_z = 2 * lax.rem(upper + 1, 2) + lax.rem(upper + 1 + 1, 2)

    def device(z_at, core_at, second_at):
        return {"first": 2 * z_at + core_at, "second": second_at}

    scope = jax.named_scope
    barrier = pltpu.get_barrier_semaphore()

    def greet(z_at, core_at, second_at):
        pl.semaphore_signal(
            barrier, inc=1, device_id=device(z_at, core_at, second_at), device_id_type=MESH
        )

    with scope("sig"):
        greet(z, 1 - core, second)
        for c in range(2):

            @pl.when(from_own)
            def _():
                greet(z, c, x_second)

            @pl.when(jnp.logical_not(from_own))
            def _():
                greet(z, c, y_second)
                greet(z, c, xy_second)

        @pl.when(jnp.logical_and(crossing, inner))
        def _():
            greet(near_z, 1, second)

        greet(near_z, 0, second)
        greet(cross_z, 1, second)

    loads = [
        pltpu.make_async_copy(src, dst, in_sem.at[n])
        for n, (src, dst) in enumerate((
            (x_hbm, x_ref), (in_gain_hbm, in_gain_ref), (left_w_hbm, left_w_ref), (right_w_hbm, right_w_ref),
            (gate_w_hbm, gate_w_ref), (mid_gain_hbm, mid_gain_ref), (out_w_hbm, out_w_ref),
        ))
    ]
    for load in loads:
        load.start()
    with scope("loadx"):
        loads[0].wait()
    with scope("loadw"):
        loads[1].wait()
        loads[2].wait()

    target = lax.rem(side + upper, 2)

    def left_copy(t, c):
        return pltpu.make_async_remote_copy(
            src_ref=lsend.at[c],
            dst_ref=lrecv.at[t % 2, core, c],
            send_sem=lsend_sem.at[t, c],
            recv_sem=lrecv_sem.at[t % 2, core, c],
            device_id=device(z, target, (second, x_second, y_second, xy_second)[t]),
            device_id_type=MESH,
        )

    with scope("left"):
        x = x_ref[...].astype(jnp.float32)
        ready = []
        for c in range(pieces):
            lump_of = jnp.concatenate(
                [x[k * cols + c * PIECE : k * cols + (c + 1) * PIECE, :] for k in range(rows)], axis=0
            )
            ready.append(norm_channels(lump_of, in_gain_ref[...]).astype(jnp.bfloat16))
            left = dot(ready[c], left_w_ref[...]).astype(jnp.bfloat16)
            lsend[c] = left

    with scope("bar"):
        pl.semaphore_wait(
            barrier,
            jnp.where(level, 6, jnp.where(outer, 5, 8)).astype(jnp.int32),
        )

    @pl.when(target != core)
    def _():
        for c in range(pieces):
            left_copy(0, c).start()

    for c in range(pieces):
        for t in (2, 1, 3):
            left_copy(t, c).start()

    with scope("right"):
        loads[3].wait()
        ready = jnp.concatenate(ready, axis=0)
        right = dot(ready, right_w_ref[...]).astype(jnp.bfloat16)
        rboth[core] = right

    right_copy = pltpu.make_async_remote_copy(
        src_ref=rboth.at[core],
        dst_ref=rboth.at[core],
        send_sem=rsend_sem,
        recv_sem=rrecv_sem,
        device_id=device(z, 1 - core, second),
        device_id_type=MESH,
    )
    right_copy.start()
    with scope("gate"):
        loads[4].wait()
        gates = jax.nn.sigmoid(dot(ready, gate_w_ref[...]))
        for c in range(pieces):
            for k in range(rows):
                at = c * lump + k * PIECE
                gate[k * cols + c * PIECE : k * cols + (c + 1) * PIECE, :] = gates[at : at + PIECE, :]
        loads[5].wait()
        loads[6].wait()

    with scope("rwait"):
        right_copy.wait_recv()
    with scope("r32"):
        for q in range(2):
            right32[q] = rboth[q].astype(jnp.float32)

    def send(j, n, slot, to):
        return pltpu.make_async_remote_copy(
            src_ref=psend.at[j, n],
            dst_ref=inbox.at[slot],
            send_sem=psend_sem.at[j, n],
            recv_sem=inbox_sem.at[slot],
            device_id=to,
            device_id_type=MESH,
        )

    near_at, cross_at, own_at = 2 * chunks, 2 * chunks + per_core, 2 * chunks + 2 * per_core
    near_early = jnp.logical_and(upper == side, parity != lax.rem(z, 2))
    held_back = jnp.logical_and(outer, jnp.logical_not(near_early))

    def relay_copy(j, n):
        return send(j, n, j * chunks + n, device(near_z, 1, second))

    def near_copy(j, n):
        return send(j, n, near_at + n % per_core, device(near_z, n // per_core, second))

    def cross_copy(j, n):
        return send(j, n, cross_at + n % per_core, device(planes_of[j], n // per_core, second))

    def own_copy(j, n):
        return send(j, n, own_at + n % per_core, device(z, 1, second))

    def block(j, c):
        with scope(f"wl{j}{c}"):
            for q in range(2):
                mine = jnp.logical_and(from_own, core == q) if j == 0 else None

                def arrived():
                    pltpu.make_async_remote_copy(
                        src_ref=lsend.at[c],
                        dst_ref=lrecv.at[j, q, c],
                        send_sem=lsend_sem.at[0, c],
                        recv_sem=lrecv_sem.at[j, q, c],
                        device_id=device(z, 1 - core, second),
                        device_id_type=MESH,
                    ).wait_recv()
                    left32[c, q] = lrecv[j, q, c].astype(jnp.float32)

                if j:
                    arrived()
                else:
                    pl.when(jnp.logical_not(mine))(arrived)

                    @pl.when(mine)
                    def _():
                        left32[c, q] = lsend[c].astype(jnp.float32)

        with scope(f"block{j}{c}"):
            for part in range(per_piece):
                n = c * per_piece + part
                sums = tuple(jnp.zeros((cols, x_ref.shape[1]), jnp.float32) for _ in range(CHUNK))
                for q in range(2):

                    def body(k, sums):
                        at = pl.multiple_of(k * PIECE, PIECE)
                        r = jnp.concatenate(
                            [right32[q, pl.ds(p * lump + at, PIECE), :] for p in range(pieces)], axis=0
                        )
                        return tuple(
                            total + left32[c, q, pl.ds(at + part * CHUNK + i, 1), :] * r
                            for i, total in enumerate(sums)
                        )

                    sums = lax.fori_loop(0, rows, body, sums, unroll=True)
                total = jnp.concatenate(sums, axis=0)

                @pl.when(jnp.logical_and(crossing, inner))
                def _():
                    part32[j, n] = total

                psend[j, n] = total.astype(jnp.bfloat16)

                @pl.when(jnp.logical_and(crossing, outer))
                def _():
                    relay_copy(j, n).start()

                @pl.when(is_own[j])
                def _():
                    if n < per_core:
                        inbox[own_at + n] = psend[j, n]
                    else:
                        own_copy(j, n).start()

                @pl.when(jnp.logical_and(is_near[j], jnp.logical_not(held_back)))
                def _():
                    near_copy(j, n).start()

    @pl.when(from_own)
    def _():
        for j in range(2):
            for c in range(pieces):
                block(j, c)

    @pl.when(jnp.logical_not(from_own))
    def _():
        for c in range(pieces):
            for j in range(2):
                block(j, c)

    everything = [
        (j, c * per_piece + part) for c in range(pieces) for j in range(2) for part in range(per_piece)
    ]
    with scope("relay"):

        @pl.when(jnp.logical_and(crossing, inner))
        def _():
            for j, n in everything:
                relay_copy(j, n).wait_recv()
                total = part32[j, n] + inbox[j * chunks + n].astype(jnp.float32)
                psend[j, n] = total.astype(jnp.bfloat16)
                cross_copy(j, n).start()

    with scope("held"):

        @pl.when(held_back)
        def _():
            @pl.when(crossing)
            def _():
                for j, n in everything:
                    relay_copy(j, n).wait_send()
                pl.semaphore_signal(go_sem, inc=1, device_id=device(z, 0, second), device_id_type=MESH)

            @pl.when(level)
            def _():
                pl.semaphore_wait(go_sem, 1)
                for j in range(2):

                    @pl.when(is_near[j])
                    def _():
                        for n in range(chunks):
                            near_copy(j, n).start()

    count = rows * 2 * planes
    for c in range(per_core):
        with scope(f"own{c}"):

            @pl.when(crossing)
            def _():
                own_copy(0, c).wait_recv()

        with scope(f"near{c}"):
            near_copy(0, c).wait_recv()
    for group in (range(per_core - 1), (per_core - 1,)):
        with scope(f"cross{group[0]}"):
            for c in group:
                cross_copy(0, c).wait_recv()
        with scope(f"final{group[0]}"):
            total = jnp.concatenate(
                [
                    inbox[own_at + c].astype(jnp.float32)
                    + inbox[near_at + c].astype(jnp.float32)
                    + inbox[cross_at + c].astype(jnp.float32)
                    for c in group
                ],
                axis=0,
            )
            mixed = (total * count ** (-0.5)).astype(jnp.bfloat16)
            scaled = norm_channels(mixed.astype(jnp.float32), mid_gain_ref[...]).astype(jnp.bfloat16)
            at = slice(group[0] * size, (group[-1] + 1) * size)
            out_ref[at, :] = (dot(scaled, out_w_ref[...]) * gate[at, :]).astype(jnp.bfloat16)

    with scope("drain"):
        for t in (1, 2, 3):
            for c in range(pieces):
                left_copy(t, c).wait_send()

        @pl.when(target != core)
        def _():
            for c in range(pieces):
                left_copy(0, c).wait_send()

        right_copy.wait_send()

        @pl.when(jnp.logical_and(crossing, jnp.logical_not(held_back)))
        def _():
            for j, n in everything:
                relay_copy(j, n).wait_send()

        @pl.when(level)
        def _():
            for j, n in everything:
                if n < per_core:

                    @pl.when(is_near[j])
                    def _():
                        near_copy(j, n).wait_send()

                else:
                    near_copy(j, n).wait_send()


def triangle(planes, lines, pair_rows, in_gain, left_weight, right_weight, mid_gain, out_weight, out_gate):
    rows, cols, width = pair_rows.shape
    mix = left_weight.shape[1]
    pairs, pieces, chunks, size = rows * cols, cols // PIECE, cols // CHUNK, CHUNK * cols
    lump = rows * PIECE
    slots = 2 * chunks + 3 * (chunks // 2)
    anywhere = pl.BlockSpec(memory_space=pl.ANY)
    bf16, f32 = jnp.bfloat16, jnp.float32
    out = pl.pallas_call(
        functools.partial(triangle_kernel, rows, cols, planes, lines),
        out_shape=pltpu.VMEM((pairs, width), bf16),
        in_specs=[anywhere] * 7,
        out_specs=pl.BlockSpec(memory_space=pltpu.VMEM),
        scratch_shapes=[
            pltpu.VMEM((pairs, width), bf16),
            pltpu.VMEM((1, width), f32),
            pltpu.VMEM((width, mix), bf16),
            pltpu.VMEM((width, mix), bf16),
            pltpu.VMEM((1, mix), f32),
            pltpu.VMEM((mix, width), bf16),
            pltpu.VMEM((width, width), bf16),
            pltpu.VMEM((pieces, lump, mix), bf16),
            pltpu.VMEM((2, 2, pieces, lump, mix), bf16),
            pltpu.VMEM((2, pairs, mix), bf16),
            pltpu.VMEM((pieces, 2, lump, mix), f32),
            pltpu.VMEM((2, pairs, mix), f32),
            pltpu.VMEM((2, chunks, size, mix), bf16),
            pltpu.VMEM((2, chunks, size, mix), f32),
            pltpu.VMEM((slots, size, mix), bf16),
            pltpu.VMEM((pairs, width), f32),
            pltpu.SemaphoreType.DMA((7,)),
            pltpu.SemaphoreType.DMA((lines, pieces)),
            pltpu.SemaphoreType.DMA((2, 2, pieces)),
            pltpu.SemaphoreType.DMA,
            pltpu.SemaphoreType.DMA,
            pltpu.SemaphoreType.DMA((2, chunks)),
            pltpu.SemaphoreType.DMA((slots,)),
            pltpu.SemaphoreType.REGULAR,
        ],
        compiler_params=pltpu.CompilerParams(collective_id=0, has_side_effects=True),
    )(
        pair_rows.reshape(pairs, width), in_gain.reshape(1, width), left_weight, right_weight,
        mid_gain.reshape(1, mix), out_weight, out_gate,
    )
    return out.reshape(rows, cols, width)


def shards(pair_rows, in_gain, left_weight, right_weight, mid_gain, out_weight, out_gate):
    ready = norm_channels(pair_rows.astype(jnp.float32), in_gain).astype(jnp.bfloat16)
    ready = lax.optimization_barrier(ready)
    left = jnp.einsum("ijc,cd->ijd", ready, left_weight, preferred_element_type=jnp.float32)
    right = jnp.einsum("ijc,cd->ijd", ready, right_weight, preferred_element_type=jnp.float32)
    left, right = left.astype(jnp.bfloat16), right.astype(jnp.bfloat16)
    count = pair_rows.shape[0] * lax.axis_size("first")
    left_lines, right_lines = (
        lax.all_to_all(left, "first", split_axis=2, concat_axis=0, tiled=True),
        lax.all_to_all(right, "first", split_axis=2, concat_axis=0, tiled=True),
    )
    strip = jnp.einsum(
        "kid,kjd->ijd",
        lax.all_gather(left_lines, "second", axis=1, tiled=True),
        right_lines,
        preferred_element_type=jnp.float32,
    )
    strip = (strip * count ** (-0.5)).astype(jnp.bfloat16)
    mixed = lax.all_to_all(strip, "first", split_axis=0, concat_axis=2, tiled=True)
    scaled = norm_channels(mixed.astype(jnp.float32), mid_gain).astype(jnp.bfloat16)
    scaled = lax.optimization_barrier(scaled)
    gate = jax.nn.sigmoid(
        jnp.einsum("ijc,cd->ijd", ready, out_gate, preferred_element_type=jnp.float32)
    )
    return (
        jnp.einsum("ijd,dc->ijc", scaled, out_weight, preferred_element_type=jnp.float32) * gate
    ).astype(jnp.bfloat16)


def solution(mesh):
    in_specs = (P("first", "second", None), P(), P(), P(), P(), P(), P())
    out_specs = P("first", "second", None)
    planes, lines = mesh.shape["first"] // 2, mesh.shape["second"]
    if planes == lines == 4:
        body = functools.partial(triangle, planes, lines)
    else:
        body = shards
    return jax.shard_map(body, mesh=mesh, in_specs=in_specs, out_specs=out_specs, check_vma=False)
```

time: 16.6 us -> 15.8 us (0.952)
  the two profiles are of different devices: /device:TPU:0 before, /device:TPU:1 now
where the time goes in v3:
time: 15.8 us; the launch traced here: 15.6 us
  Pallas kernels  15 us (95%)
  local copies, waits for them, and re-layouts  0.64 us (4%)
    pallas_call x1, Pallas kernels, triangle(): pl.pallas_call(functools.partial(triangle_kernel, rows, cols, planes, lin...  15 us
    unnamed x1, local copies, waits for them, and re-layouts  0.64 us

profile of v3, /device:TPU:1, one launch (start us, length us, event | category | flops | bytes accessed | tf_op | source)
XLA Modules:
  0.0 15.6 jit_solution(9581730519193248912)
XLA Ops:
  0.0 15.0 %shard_map.73 = bf16[288,128]{1,0:T(8,128)(2,1)S(1)} custom-call(bf16[288,128]{1,0:T(8,128)(2,1)} %bitcast.5, f32[1,128]{1,0:T(1,128)} %bitcast.6, bf16[128,128]{1,0:T(8,128)(2,1)} %left_w_hbm.1, bf16[128,128]{1,0:T(8,128)(2,1)} %right_w_hbm.1, f32[1,128]{1,0:T(1,128)} %bitcast.7, bf16[128,128]{1,0:T(8,128)(2,1)} %out_w_hbm.1, bf16[128,128]{1,0:T(8,128)(2,1)} %gate_w_hbm.1), custom_call_target="tpu_custom_call" | custom-call | tf_op jit(solution)/shard_map/pallas_call | solution.py:381
  15.0 0.6 %copy.9 = bf16[12,24,128]{2,1,0:T(8,128)(2,1)} copy(bf16[12,24,128]{2,1,0:T(8,128)(2,1)S(1)} %bitcast.4) | data formatting | bytes 147456

commit v4 on v3

--- a/solution.py
+++ b/solution.py
@@ -31,13 +31,37 @@
     return index + 1 - 2 * lax.rem(index, 2)
 
 
-def triangle_kernel(
+def centre(values, channel_gain):
+    centred = values - jnp.mean(values, axis=-1, keepdims=True)
+    scale = lax.rsqrt(jnp.mean(centred * centred, axis=-1, keepdims=True) + 1e-05)
+    return (centred * channel_gain).astype(jnp.bfloat16), scale
+
+
+def triangle_kernel(rows, cols, planes, lines, *refs):
+    pieces, chunks = cols // PIECE, cols // CHUNK
+    pl.run_scoped(
+        functools.partial(triangle_steps, rows, cols, planes, lines, *refs),
+        pltpu.SemaphoreType.DMA((6 + pieces,)),
+        pltpu.SemaphoreType.DMA((lines, pieces)),
+        pltpu.SemaphoreType.DMA((2, 2, pieces)),
+        pltpu.SemaphoreType.DMA,
+        pltpu.SemaphoreType.DMA,
+        pltpu.SemaphoreType.DMA((2, chunks)),
+        pltpu.SemaphoreType.DMA((2 * chunks + 3 * (chunks // 2),)),
+        pltpu.SemaphoreType.REGULAR,
+        pltpu.SemaphoreType.REGULAR,
+        pltpu.SemaphoreType.REGULAR,
+        pltpu.SemaphoreType.REGULAR,
+    )
+
+
+def triangle_steps(
     rows, cols, planes, lines,
     x_hbm, in_gain_hbm, left_w_hbm, right_w_hbm, mid_gain_hbm, out_w_hbm, gate_w_hbm,
     out_ref,
     x_ref, in_gain_ref, left_w_ref, right_w_ref, mid_gain_ref, out_w_ref, gate_w_ref,
     lsend, lrecv, rboth, left32, right32, psend, part32, inbox, gate,
-    in_sem, lsend_sem, lrecv_sem, rsend_sem, rrecv_sem, psend_sem, inbox_sem, go_sem,
+    in_sem, lsend_sem, lrecv_sem, rsend_sem, rrecv_sem, psend_sem, inbox_sem, go_sem, across_sem, cross_sem, near_sem,
 ):
     first, second = lax.axis_index("first"), lax.axis_index("second")
     z, core = lax.div(first, 2), lax.rem(first, 2)
@@ -71,6 +95,10 @@
             barrier, inc=1, device_id=device(z_at, core_at, second_at), device_id_type=MESH
         )
 
+    target = lax.rem(side + upper, 2)
+    early = jnp.logical_and(crossing, jnp.logical_and(inner, upper == 0))
+    even = lax.rem(z, 2) == 0
+
     with scope("sig"):
         greet(z, 1 - core, second)
         for c in range(2):
@@ -82,31 +110,84 @@
             @pl.when(jnp.logical_not(from_own))
             def _():
                 greet(z, c, y_second)
-                greet(z, c, xy_second)
-
-        @pl.when(jnp.logical_and(crossing, inner))
-        def _():
-            greet(near_z, 1, second)
-
-        greet(near_z, 0, second)
-        greet(cross_z, 1, second)
+
+        @pl.when(side == 0)
+        def _():
+            greet(z, target, xy_second)
+
+            @pl.when(jnp.logical_not(from_own))
+            def _():
+                for c in range(2):
+                    greet(z, c, xy_second)
+
+        @pl.when(even)
+        def _():
+            greet(near_z, 0, second)
+
+            @pl.when(level)
+            def _():
+                for c in range(2):
+                    greet(near_z, c, second)
+
+            @pl.when(crossing)
+            def _():
+                greet(near_z, 1, second)
+
+        @pl.when(upper == 0)
+        def _():
+            greet(cross_z, 1, second)
+
+        @pl.when(early)
+        def _():
+            for dz in range(half):
+                for c in range(2):
+                    greet(half + dz, c, second)
 
     loads = [
         pltpu.make_async_copy(src, dst, in_sem.at[n])
         for n, (src, dst) in enumerate((
-            (x_hbm, x_ref), (in_gain_hbm, in_gain_ref), (left_w_hbm, left_w_ref), (right_w_hbm, right_w_ref),
+            (in_gain_hbm, in_gain_ref), (left_w_hbm, left_w_ref),
+            *((x_hbm.at[:, pl.ds(c * PIECE, PIECE), :], x_ref.at[c]) for c in range(pieces)),
+            (right_w_hbm, right_w_ref),
             (gate_w_hbm, gate_w_ref), (mid_gain_hbm, mid_gain_ref), (out_w_hbm, out_w_ref),
         ))
     ]
     for load in loads:
         load.start()
-    with scope("loadx"):
-        loads[0].wait()
-    with scope("loadw"):
-        loads[1].wait()
-        loads[2].wait()
-
-    target = lax.rem(side + upper, 2)
+    def meet():
+        signals = (
+            3
+            + jnp.where(even, 0, 1 + jnp.where(level, 2, 1))
+            + jnp.where(jnp.logical_and(crossing, z == half), 2 * half, 0)
+            + jnp.where(side == 0, 0, 1 + jnp.where(from_own, 0, 2))
+            + upper
+        )
+        pl.semaphore_wait(barrier, signals.astype(jnp.int32))
+
+        def answer(semaphore, z_at, core_at, second_at):
+            pl.semaphore_signal(
+                semaphore, inc=1, device_id=device(z_at, core_at, second_at), device_id_type=MESH
+            )
+
+        @pl.when(jnp.logical_and(side == 1, jnp.logical_not(from_own)))
+        def _():
+            for c in range(2):
+                answer(across_sem, z, c, xy_second)
+
+        @pl.when(jnp.logical_not(even))
+        def _():
+            answer(near_sem, near_z, 0, second)
+
+        @pl.when(early)
+        def _():
+            answer(near_sem, near_z, 1, second)
+
+        @pl.when(upper == 1)
+        def _():
+            answer(cross_sem, cross_z, 1, second)
+
+    with scope("bar"):
+        pl.when(side == 1)(meet)
 
     def left_copy(t, c):
         return pltpu.make_async_remote_copy(
@@ -118,36 +199,32 @@
             device_id_type=MESH,
         )
 
-    with scope("left"):
-        x = x_ref[...].astype(jnp.float32)
-        ready = []
-        for c in range(pieces):
-            lump_of = jnp.concatenate(
-                [x[k * cols + c * PIECE : k * cols + (c + 1) * PIECE, :] for k in range(rows)], axis=0
-            )
-            ready.append(norm_channels(lump_of, in_gain_ref[...]).astype(jnp.bfloat16))
-            left = dot(ready[c], left_w_ref[...]).astype(jnp.bfloat16)
-            lsend[c] = left
-
-    with scope("bar"):
-        pl.semaphore_wait(
-            barrier,
-            jnp.where(level, 6, jnp.where(outer, 5, 8)).astype(jnp.int32),
-        )
-
-    @pl.when(target != core)
-    def _():
-        for c in range(pieces):
+    with scope("load"):
+        loads[0].wait()
+        loads[1].wait()
+
+    ready, scales = [], []
+    for c in range(pieces):
+        with scope(f"left{c}"):
+            loads[2 + c].wait()
+            x = x_ref[c].astype(jnp.float32).reshape(lump, x_ref.shape[-1])
+            for list_of, value in zip((ready, scales), centre(x, in_gain_ref[...])):
+                list_of.append(value)
+            lsend[c] = (dot(ready[c], left_w_ref[...]) * scales[c]).astype(jnp.bfloat16)
+        if c == 0:
+            with scope("bar0"):
+                pl.when(side == 0)(meet)
+        for t in (2, 1):
+            left_copy(t, c).start()
+
+        @pl.when(target != core)
+        def _():
             left_copy(0, c).start()
 
-    for c in range(pieces):
-        for t in (2, 1, 3):
-            left_copy(t, c).start()
-
     with scope("right"):
-        loads[3].wait()
-        ready = jnp.concatenate(ready, axis=0)
-        right = dot(ready, right_w_ref[...]).astype(jnp.bfloat16)
+        loads[pieces + 2].wait()
+        ready, scales = (jnp.concatenate(list_of, axis=0) for list_of in (ready, scales))
+        right = (dot(ready, right_w_ref[...]) * scales).astype(jnp.bfloat16)
         rboth[core] = right
 
     right_copy = pltpu.make_async_remote_copy(
@@ -159,15 +236,22 @@
         device_id_type=MESH,
     )
     right_copy.start()
+    with scope("across"):
+        @pl.when(side == 0)
+        def _():
+            pl.semaphore_wait(across_sem, 1)
+
+        for c in range(pieces):
+            left_copy(3, c).start()
     with scope("gate"):
-        loads[4].wait()
-        gates = jax.nn.sigmoid(dot(ready, gate_w_ref[...]))
+        loads[pieces + 3].wait()
+        gates = jax.nn.sigmoid(dot(ready, gate_w_ref[...]) * scales)
         for c in range(pieces):
             for k in range(rows):
                 at = c * lump + k * PIECE
                 gate[k * cols + c * PIECE : k * cols + (c + 1) * PIECE, :] = gates[at : at + PIECE, :]
-        loads[5].wait()
-        loads[6].wait()
+        loads[pieces + 4].wait()
+        loads[pieces + 5].wait()
 
     with scope("rwait"):
         right_copy.wait_recv()
@@ -229,7 +313,7 @@
         with scope(f"block{j}{c}"):
             for part in range(per_piece):
                 n = c * per_piece + part
-                sums = tuple(jnp.zeros((cols, x_ref.shape[1]), jnp.float32) for _ in range(CHUNK))
+                sums = tuple(jnp.zeros((cols, x_ref.shape[-1]), jnp.float32) for _ in range(CHUNK))
                 for q in range(2):
 
                     def body(k, sums):
@@ -266,38 +350,43 @@
                 def _():
                     near_copy(j, n).start()
 
-    @pl.when(from_own)
-    def _():
-        for j in range(2):
-            for c in range(pieces):
-                block(j, c)
-
-    @pl.when(jnp.logical_not(from_own))
-    def _():
+    with scope("nearbar"):
+
+        @pl.when(jnp.logical_and(even, level))
+        def _():
+            pl.semaphore_wait(near_sem, 2)
+
+        @pl.when(jnp.logical_and(z == 0, crossing))
+        def _():
+            pl.semaphore_wait(near_sem, 1)
+
+    for j in range(2):
         for c in range(pieces):
-            for j in range(2):
-                block(j, c)
-
-    everything = [
-        (j, c * per_piece + part) for c in range(pieces) for j in range(2) for part in range(per_piece)
-    ]
+            block(j, c)
+
+    by_plane = [(j, n) for j in range(2) for n in range(chunks)]
     with scope("relay"):
 
+        @pl.when(early)
+        def _():
+            pl.semaphore_wait(cross_sem, 2 * half)
+
         @pl.when(jnp.logical_and(crossing, inner))
         def _():
-            for j, n in everything:
+            for j, n in by_plane:
                 relay_copy(j, n).wait_recv()
                 total = part32[j, n] + inbox[j * chunks + n].astype(jnp.float32)
                 psend[j, n] = total.astype(jnp.bfloat16)
                 cross_copy(j, n).start()
 
+    first_sends, last_sends = by_plane[: -chunks // 2], by_plane[-chunks // 2 :]
     with scope("held"):
 
         @pl.when(held_back)
         def _():
             @pl.when(crossing)
             def _():
-                for j, n in everything:
+                for j, n in first_sends:
                     relay_copy(j, n).wait_send()
                 pl.semaphore_signal(go_sem, inc=1, device_id=device(z, 0, second), device_id_type=MESH)
 
@@ -321,24 +410,19 @@
 
         with scope(f"near{c}"):
             near_copy(0, c).wait_recv()
-    for group in (range(per_core - 1), (per_core - 1,)):
-        with scope(f"cross{group[0]}"):
-            for c in group:
-                cross_copy(0, c).wait_recv()
-        with scope(f"final{group[0]}"):
-            total = jnp.concatenate(
-                [
-                    inbox[own_at + c].astype(jnp.float32)
-                    + inbox[near_at + c].astype(jnp.float32)
-                    + inbox[cross_at + c].astype(jnp.float32)
-                    for c in group
-                ],
-                axis=0,
-            )
-            mixed = (total * count ** (-0.5)).astype(jnp.bfloat16)
-            scaled = norm_channels(mixed.astype(jnp.float32), mid_gain_ref[...]).astype(jnp.bfloat16)
-            at = slice(group[0] * size, (group[-1] + 1) * size)
-            out_ref[at, :] = (dot(scaled, out_w_ref[...]) * gate[at, :]).astype(jnp.bfloat16)
+    with scope("sum"):
+        for c in range(per_core):
+            part32[0, c] = inbox[own_at + c].astype(jnp.float32) + inbox[near_at + c].astype(jnp.float32)
+    with scope("cross"):
+        for c in range(per_core):
+            cross_copy(0, c).wait_recv()
+    with scope("final"):
+        total = jnp.concatenate(
+            [part32[0, c] + inbox[cross_at + c].astype(jnp.float32) for c in range(per_core)], axis=0
+        )
+        mixed = (total * count ** (-0.5)).astype(jnp.bfloat16)
+        scaled, scale = centre(mixed.astype(jnp.float32), mid_gain_ref[...])
+        out_ref[...] = (dot(scaled, out_w_ref[...]) * (gate[...] * scale)).astype(jnp.bfloat16)
 
     with scope("drain"):
         for t in (1, 2, 3):
@@ -352,14 +436,19 @@
 
         right_copy.wait_send()
 
-        @pl.when(jnp.logical_and(crossing, jnp.logical_not(held_back)))
-        def _():
-            for j, n in everything:
+        @pl.when(crossing)
+        def _():
+            for j, n in last_sends:
                 relay_copy(j, n).wait_send()
 
+            @pl.when(jnp.logical_not(held_back))
+            def _():
+                for j, n in first_sends:
+                    relay_copy(j, n).wait_send()
+
         @pl.when(level)
         def _():
-            for j, n in everything:
+            for j, n in by_plane:
                 if n < per_core:
 
                     @pl.when(is_near[j])
@@ -384,7 +473,7 @@
         in_specs=[anywhere] * 7,
         out_specs=pl.BlockSpec(memory_space=pltpu.VMEM),
         scratch_shapes=[
-            pltpu.VMEM((pairs, width), bf16),
+            pltpu.VMEM((pieces, rows, PIECE, width), bf16),
             pltpu.VMEM((1, width), f32),
             pltpu.VMEM((width, mix), bf16),
             pltpu.VMEM((width, mix), bf16),
@@ -400,18 +489,10 @@
             pltpu.VMEM((2, chunks, size, mix), f32),
             pltpu.VMEM((slots, size, mix), bf16),
             pltpu.VMEM((pairs, width), f32),
-            pltpu.SemaphoreType.DMA((7,)),
-            pltpu.SemaphoreType.DMA((lines, pieces)),
-            pltpu.SemaphoreType.DMA((2, 2, pieces)),
-            pltpu.SemaphoreType.DMA,
-            pltpu.SemaphoreType.DMA,
-            pltpu.SemaphoreType.DMA((2, chunks)),
-            pltpu.SemaphoreType.DMA((slots,)),
-            pltpu.SemaphoreType.REGULAR,
         ],
         compiler_params=pltpu.CompilerParams(collective_id=0, has_side_effects=True),
     )(
-        pair_rows.reshape(pairs, width), in_gain.reshape(1, width), left_weight, right_weight,
+        pair_rows, in_gain.reshape(1, width), left_weight, right_weight,
         mid_gain.reshape(1, mix), out_weight, out_gate,
     )
     return out.reshape(rows, cols, width)

time: 15.8 us -> 14.5 us (0.918)
  the two profiles are of different devices: /device:TPU:1 before, /device:TPU:13 now
where the time goes in v4:
time: 14.5 us; the launch traced here: 14.3 us
  Pallas kernels  13.7 us (94%)
  local copies, waits for them, and re-layouts  0.64 us (4%)
    pallas_call x1, Pallas kernels, triangle(): pl.pallas_call(functools.partial(triangle_kernel, rows, cols, planes, lin...  13.7 us
    unnamed x1, local copies, waits for them, and re-layouts  0.64 us

profile of v4, /device:TPU:13, one launch (start us, length us, event | category | flops | bytes accessed | tf_op | source)
XLA Modules:
  0.0 14.3 jit_solution(15838162097280720259)
XLA Ops:
  0.0 13.7 %shard_map.73 = bf16[288,128]{1,0:T(8,128)(2,1)S(1)} custom-call(bf16[12,24,128]{2,1,0:T(8,128)(2,1)} %refs_0_.1, f32[1,128]{1,0:T(1,128)} %bitcast.4, bf16[128,128]{1,0:T(8,128)(2,1)} %refs_2_.1, bf16[128,128]{1,0:T(8,128)(2,1)} %refs_3_.1, f32[1,128]{1,0:T(1,128)} %bitcast.5, bf16[128,128]{1,0:T(8,128)(2,1)} %refs_5_.1, bf16[128,128]{1,0:T(8,128)(2,1)} %refs_6_.1), custom_call_target="tpu_custom_call" | custom-call | tf_op jit(solution)/shard_map/pallas_call | solution.py:470
  13.7 0.6 %copy.9 = bf16[12,24,128]{2,1,0:T(8,128)(2,1)} copy(bf16[12,24,128]{2,1,0:T(8,128)(2,1)S(1)} %bitcast.3) | data formatting | bytes 147456

commit v5 on v4

--- a/solution.py
+++ b/solution.py
@@ -98,6 +98,8 @@
     target = lax.rem(side + upper, 2)
     early = jnp.logical_and(crossing, jnp.logical_and(inner, upper == 0))
     even = lax.rem(z, 2) == 0
+    last_column = second == lines - 1
+    slow_column = second == half
 
     with scope("sig"):
         greet(z, 1 - core, second)
@@ -187,7 +189,7 @@
             answer(cross_sem, cross_z, 1, second)
 
     with scope("bar"):
-        pl.when(side == 1)(meet)
+        pl.when(last_column)(meet)
 
     def left_copy(t, c):
         return pltpu.make_async_remote_copy(
@@ -202,6 +204,14 @@
     with scope("load"):
         loads[0].wait()
         loads[1].wait()
+
+    def send_left(c):
+        for t in (2, 1):
+            left_copy(t, c).start()
+
+        @pl.when(target != core)
+        def _():
+            left_copy(0, c).start()
 
     ready, scales = [], []
     for c in range(pieces):
@@ -214,18 +224,23 @@
         if c == 0:
             with scope("bar0"):
                 pl.when(side == 0)(meet)
-        for t in (2, 1):
-            left_copy(t, c).start()
-
-        @pl.when(target != core)
-        def _():
-            left_copy(0, c).start()
+
+        @pl.when(jnp.logical_not(slow_column))
+        def _():
+            send_left(c)
 
     with scope("right"):
         loads[pieces + 2].wait()
         ready, scales = (jnp.concatenate(list_of, axis=0) for list_of in (ready, scales))
         right = (dot(ready, right_w_ref[...]) * scales).astype(jnp.bfloat16)
         rboth[core] = right
+    with scope("bar2"):
+
+        @pl.when(slow_column)
+        def _():
+            meet()
+            for c in range(pieces):
+                send_left(c)
 
     right_copy = pltpu.make_async_remote_copy(
         src_ref=rboth.at[core],

time: 14.5 us -> 14.2 us (0.979)
  Pallas kernels: 13.7 us -> 13.3 us
    pallas_call x1, Pallas kernels: 13.7 us -> 13.3 us  [triangle(): pl.pallas_call(functools.partial(triangle_kernel, rows, cols, planes, lin...]
where the time goes in v5:
time: 14.2 us; the launch traced here: 13.9 us
  Pallas kernels  13.3 us (94%)
  local copies, waits for them, and re-layouts  0.64 us (5%)
    pallas_call x1, Pallas kernels, triangle(): pl.pallas_call(functools.partial(triangle_kernel, rows, cols, planes, lin...  13.3 us
    unnamed x1, local copies, waits for them, and re-layouts  0.64 us

profile of v5, /device:TPU:13, one launch (start us, length us, event | category | flops | bytes accessed | tf_op | source)
XLA Modules:
  0.0 13.9 jit_solution(735110990774210856)
XLA Ops:
  0.0 13.3 %shard_map.73 = bf16[288,128]{1,0:T(8,128)(2,1)S(1)} custom-call(bf16[12,24,128]{2,1,0:T(8,128)(2,1)} %refs_0_.1, f32[1,128]{1,0:T(1,128)} %bitcast.4, bf16[128,128]{1,0:T(8,128)(2,1)} %refs_2_.1, bf16[128,128]{1,0:T(8,128)(2,1)} %refs_3_.1, f32[1,128]{1,0:T(1,128)} %bitcast.5, bf16[128,128]{1,0:T(8,128)(2,1)} %refs_5_.1, bf16[128,128]{1,0:T(8,128)(2,1)} %refs_6_.1), custom_call_target="tpu_custom_call" | custom-call | tf_op jit(solution)/shard_map/pallas_call | solution.py:485
  13.3 0.6 %copy.9 = bf16[12,24,128]{2,1,0:T(8,128)(2,1)} copy(bf16[12,24,128]{2,1,0:T(8,128)(2,1)S(1)} %bitcast.3) | data formatting | bytes 147456

commit v6 on v5

--- a/solution.py
+++ b/solution.py
@@ -24,7 +24,8 @@
 
 
 PIECE = 8
-CHUNK = 4
+CHUNK = 2
+DIRECT = 2
 
 
 def other(index):
@@ -47,7 +48,7 @@
         pltpu.SemaphoreType.DMA,
         pltpu.SemaphoreType.DMA,
         pltpu.SemaphoreType.DMA((2, chunks)),
-        pltpu.SemaphoreType.DMA((2 * chunks + 3 * (chunks // 2),)),
+        pltpu.SemaphoreType.DMA((2 * chunks + 4 * (chunks // 2),)),
         pltpu.SemaphoreType.REGULAR,
         pltpu.SemaphoreType.REGULAR,
         pltpu.SemaphoreType.REGULAR,
@@ -98,11 +99,17 @@
     target = lax.rem(side + upper, 2)
     early = jnp.logical_and(crossing, jnp.logical_and(inner, upper == 0))
     even = lax.rem(z, 2) == 0
+    far_target = jnp.logical_and(jnp.logical_and(crossing, upper == 0), lax.rem(z, 2) != parity)
     last_column = second == lines - 1
     slow_column = second == half
 
     with scope("sig"):
         greet(z, 1 - core, second)
+
+        @pl.when(far_target)
+        def _():
+            greet(planes - 1, 1, second)
+
         for c in range(2):
 
             @pl.when(from_own)
@@ -115,7 +122,7 @@
 
         @pl.when(side == 0)
         def _():
-            greet(z, target, xy_second)
+            greet(z, core, jnp.where(parity == 0, x_second, xy_second))
 
             @pl.when(jnp.logical_not(from_own))
             def _():
@@ -161,7 +168,8 @@
             3
             + jnp.where(even, 0, 1 + jnp.where(level, 2, 1))
             + jnp.where(jnp.logical_and(crossing, z == half), 2 * half, 0)
-            + jnp.where(side == 0, 0, 1 + jnp.where(from_own, 0, 2))
+            + jnp.where(jnp.logical_and(crossing, z == planes - 1), 1, 0)
+            + jnp.where(side == 0, parity, 2 - parity)
             + upper
         )
         pl.semaphore_wait(barrier, signals.astype(jnp.int32))
@@ -171,10 +179,13 @@
                 semaphore, inc=1, device_id=device(z_at, core_at, second_at), device_id_type=MESH
             )
 
-        @pl.when(jnp.logical_and(side == 1, jnp.logical_not(from_own)))
-        def _():
-            for c in range(2):
-                answer(across_sem, z, c, xy_second)
+        @pl.when(slow_column)
+        def _():
+            answer(across_sem, z, core, xy_second)
+
+        @pl.when(jnp.logical_and(side == 0, parity == 1))
+        def _():
+            answer(across_sem, z, core, x_second)
 
         @pl.when(jnp.logical_not(even))
         def _():
@@ -284,12 +295,20 @@
             device_id_type=MESH,
         )
 
-    near_at, cross_at, own_at = 2 * chunks, 2 * chunks + per_core, 2 * chunks + 2 * per_core
+    near_at, cross_at, own_at, far_at = (2 * chunks + n * per_core for n in range(4))
+    descending = jnp.logical_and(crossing, upper == 1)
+
+    def skips(j, n):
+        return j == 1 and n >= chunks - DIRECT
+
     near_early = jnp.logical_and(upper == side, parity != lax.rem(z, 2))
     held_back = jnp.logical_and(outer, jnp.logical_not(near_early))
 
     def relay_copy(j, n):
         return send(j, n, j * chunks + n, device(near_z, 1, second))
+
+    def far_copy(j, n):
+        return send(j, n, far_at + n % per_core, device(planes_of[j], 1, second))
 
     def near_copy(j, n):
         return send(j, n, near_at + n % per_core, device(near_z, n // per_core, second))
@@ -350,9 +369,19 @@
 
                 psend[j, n] = total.astype(jnp.bfloat16)
 
-                @pl.when(jnp.logical_and(crossing, outer))
+                @pl.when(jnp.logical_and(crossing, jnp.logical_and(outer, upper == 0) if skips(j, n) else outer))
                 def _():
                     relay_copy(j, n).start()
+
+                if skips(j, n):
+
+                    @pl.when(jnp.logical_and(descending, outer))
+                    def _():
+                        far_copy(j, n).start()
+
+                    @pl.when(jnp.logical_and(descending, inner))
+                    def _():
+                        cross_copy(j, n).start()
 
                 @pl.when(is_own[j])
                 def _():
@@ -389,12 +418,19 @@
         @pl.when(jnp.logical_and(crossing, inner))
         def _():
             for j, n in by_plane:
-                relay_copy(j, n).wait_recv()
-                total = part32[j, n] + inbox[j * chunks + n].astype(jnp.float32)
-                psend[j, n] = total.astype(jnp.bfloat16)
-                cross_copy(j, n).start()
-
-    first_sends, last_sends = by_plane[: -chunks // 2], by_plane[-chunks // 2 :]
+
+                def relay():
+                    relay_copy(j, n).wait_recv()
+                    total = part32[j, n] + inbox[j * chunks + n].astype(jnp.float32)
+                    psend[j, n] = total.astype(jnp.bfloat16)
+                    cross_copy(j, n).start()
+
+                if skips(j, n):
+                    pl.when(upper == 0)(relay)
+                else:
+                    relay()
+
+    first_sends, last_sends = by_plane[: -chunks // 4], by_plane[-chunks // 4 :]
     with scope("held"):
 
         @pl.when(held_back)
@@ -431,9 +467,21 @@
     with scope("cross"):
         for c in range(per_core):
             cross_copy(0, c).wait_recv()
+    with scope("far"):
+
+        @pl.when(far_target)
+        def _():
+            for c in range(per_core - DIRECT, per_core):
+                part32[0, c] = part32[0, c] + inbox[cross_at + c].astype(jnp.float32)
+                send(0, c, far_at + c, device(near_z, 0, second)).wait_recv()
+
+    last_at = [
+        (jnp.where(far_target, far_at, cross_at) if c >= per_core - DIRECT else cross_at) + c
+        for c in range(per_core)
+    ]
     with scope("final"):
         total = jnp.concatenate(
-            [part32[0, c] + inbox[cross_at + c].astype(jnp.float32) for c in range(per_core)], axis=0
+            [part32[0, c] + inbox[last_at[c]].astype(jnp.float32) for c in range(per_core)], axis=0
         )
         mixed = (total * count ** (-0.5)).astype(jnp.bfloat16)
         scaled, scale = centre(mixed.astype(jnp.float32), mid_gain_ref[...])
@@ -479,7 +527,7 @@
     mix = left_weight.shape[1]
     pairs, pieces, chunks, size = rows * cols, cols // PIECE, cols // CHUNK, CHUNK * cols
     lump = rows * PIECE
-    slots = 2 * chunks + 3 * (chunks // 2)
+    slots = 2 * chunks + 4 * (chunks // 2)
     anywhere = pl.BlockSpec(memory_space=pl.ANY)
     bf16, f32 = jnp.bfloat16, jnp.float32
     out = pl.pallas_call(

time: 14.2 us -> 14 us (0.986)
  no operation moved by 1% of the time
where the time goes in v6:
time: 14 us; the launch traced here: 13.8 us
  Pallas kernels  13.2 us (94%)
  local copies, waits for them, and re-layouts  0.64 us (5%)
    pallas_call x1, Pallas kernels, triangle(): pl.pallas_call(functools.partial(triangle_kernel, rows, cols, planes, lin...  13.2 us
    unnamed x1, local copies, waits for them, and re-layouts  0.64 us

profile of v6, /device:TPU:13, one launch (start us, length us, event | category | flops | bytes accessed | tf_op | source)
XLA Modules:
  0.0 13.8 jit_solution(17510870066400238596)
XLA Ops:
  0.0 13.2 %shard_map.73 = bf16[288,128]{1,0:T(8,128)(2,1)S(1)} custom-call(bf16[12,24,128]{2,1,0:T(8,128)(2,1)} %refs_0_.1, f32[1,128]{1,0:T(1,128)} %bitcast.4, bf16[128,128]{1,0:T(8,128)(2,1)} %refs_2_.1, bf16[128,128]{1,0:T(8,128)(2,1)} %refs_3_.1, f32[1,128]{1,0:T(1,128)} %bitcast.5, bf16[128,128]{1,0:T(8,128)(2,1)} %refs_5_.1, bf16[128,128]{1,0:T(8,128)(2,1)} %refs_6_.1), custom_call_target="tpu_custom_call" | custom-call | tf_op jit(solution)/shard_map/pallas_call | solution.py:533
  13.2 0.6 %copy.9 = bf16[12,24,128]{2,1,0:T(8,128)(2,1)} copy(bf16[12,24,128]{2,1,0:T(8,128)(2,1)S(1)} %bitcast.3) | data formatting | bytes 147456

commit v7 on v6

--- a/solution.py
+++ b/solution.py
@@ -120,14 +120,14 @@
             def _():
                 greet(z, c, y_second)
 
-        @pl.when(side == 0)
-        def _():
-            greet(z, core, jnp.where(parity == 0, x_second, xy_second))
-
-            @pl.when(jnp.logical_not(from_own))
-            def _():
-                for c in range(2):
-                    greet(z, c, xy_second)
+        @pl.when(jnp.logical_and(crossing, jnp.logical_not(last_column)))
+        def _():
+            greet(z, 1, x_second)
+
+        @pl.when(jnp.logical_and(second == 0, jnp.logical_not(from_own)))
+        def _():
+            for c in range(2):
+                greet(z, c, xy_second)
 
         @pl.when(even)
         def _():
@@ -169,7 +169,8 @@
             + jnp.where(even, 0, 1 + jnp.where(level, 2, 1))
             + jnp.where(jnp.logical_and(crossing, z == half), 2 * half, 0)
             + jnp.where(jnp.logical_and(crossing, z == planes - 1), 1, 0)
-            + jnp.where(side == 0, parity, 2 - parity)
+            + jnp.where(last_column, 1, 0)
+            + jnp.where(jnp.logical_and(crossing, second != half), 1, 0)
             + upper
         )
         pl.semaphore_wait(barrier, signals.astype(jnp.int32))
@@ -179,13 +180,9 @@
                 semaphore, inc=1, device_id=device(z_at, core_at, second_at), device_id_type=MESH
             )
 
-        @pl.when(slow_column)
-        def _():
-            answer(across_sem, z, core, xy_second)
-
-        @pl.when(jnp.logical_and(side == 0, parity == 1))
-        def _():
-            answer(across_sem, z, core, x_second)
+        @pl.when(jnp.logical_and(crossing, second != half))
+        def _():
+            answer(across_sem, z, 1, x_second)
 
         @pl.when(jnp.logical_not(even))
         def _():
@@ -263,9 +260,15 @@
     )
     right_copy.start()
     with scope("across"):
-        @pl.when(side == 0)
+        @pl.when(jnp.logical_not(last_column))
         def _():
             pl.semaphore_wait(across_sem, 1)
+
+            @pl.when(crossing)
+            def _():
+                pl.semaphore_signal(
+                    across_sem, inc=1, device_id=device(z, 0, second), device_id_type=MESH
+                )
 
         for c in range(pieces):
             left_copy(3, c).start()
@@ -298,11 +301,14 @@
     near_at, cross_at, own_at, far_at = (2 * chunks + n * per_core for n in range(4))
     descending = jnp.logical_and(crossing, upper == 1)
 
+    def waits(j, n):
+        return j == 0 and n >= per_core
+
     def skips(j, n):
         return j == 1 and n >= chunks - DIRECT
 
     near_early = jnp.logical_and(upper == side, parity != lax.rem(z, 2))
-    held_back = jnp.logical_and(outer, jnp.logical_not(near_early))
+    held_back = outer
 
     def relay_copy(j, n):
         return send(j, n, j * chunks + n, device(near_z, 1, second))
@@ -369,7 +375,13 @@
 
                 psend[j, n] = total.astype(jnp.bfloat16)
 
-                @pl.when(jnp.logical_and(crossing, jnp.logical_and(outer, upper == 0) if skips(j, n) else outer))
+                sends = jnp.logical_and(crossing, outer)
+                if skips(j, n):
+                    sends = jnp.logical_and(sends, upper == 0)
+                if waits(j, n):
+                    sends = jnp.logical_and(sends, parity == 0)
+
+                @pl.when(sends)
                 def _():
                     relay_copy(j, n).start()
 
@@ -409,6 +421,15 @@
             block(j, c)
 
     by_plane = [(j, n) for j in range(2) for n in range(chunks)]
+    by_need = sorted(by_plane, key=lambda at: waits(*at))
+    with scope("late"):
+
+        @pl.when(jnp.logical_and(jnp.logical_and(crossing, outer), parity == 1))
+        def _():
+            for j, n in by_plane:
+                if waits(j, n):
+                    relay_copy(j, n).start()
+
     with scope("relay"):
 
         @pl.when(early)
@@ -417,28 +438,36 @@
 
         @pl.when(jnp.logical_and(crossing, inner))
         def _():
-            for j, n in by_plane:
-
-                def relay():
-                    relay_copy(j, n).wait_recv()
-                    total = part32[j, n] + inbox[j * chunks + n].astype(jnp.float32)
-                    psend[j, n] = total.astype(jnp.bfloat16)
-                    cross_copy(j, n).start()
-
-                if skips(j, n):
-                    pl.when(upper == 0)(relay)
-                else:
-                    relay()
-
-    first_sends, last_sends = by_plane[: -chunks // 4], by_plane[-chunks // 4 :]
+            def relay(j, n):
+                relay_copy(j, n).wait_recv()
+                total = part32[j, n] + inbox[j * chunks + n].astype(jnp.float32)
+                psend[j, n] = total.astype(jnp.bfloat16)
+                cross_copy(j, n).start()
+
+            def relay_all(order):
+                for j, n in order:
+                    if skips(j, n):
+                        pl.when(upper == 0)(functools.partial(relay, j, n))
+                    else:
+                        relay(j, n)
+
+            pl.when(parity == 0)(lambda: relay_all(by_plane))
+            pl.when(parity == 1)(lambda: relay_all(by_need))
+
+    cuts = (by_plane, 2 * chunks - chunks // 4), (by_need, 2 * chunks - per_core)
+
+    def wait_sent(order):
+        for j, n in order:
+            near_copy(j, n).wait_send()
+
     with scope("held"):
 
         @pl.when(held_back)
         def _():
             @pl.when(crossing)
             def _():
-                for j, n in first_sends:
-                    relay_copy(j, n).wait_send()
+                for odd, (order, cut) in enumerate(cuts):
+                    pl.when(parity == odd)(functools.partial(wait_sent, order[:cut]))
                 pl.semaphore_signal(go_sem, inc=1, device_id=device(z, 0, second), device_id_type=MESH)
 
             @pl.when(level)
@@ -464,6 +493,39 @@
     with scope("sum"):
         for c in range(per_core):
             part32[0, c] = inbox[own_at + c].astype(jnp.float32) + inbox[near_at + c].astype(jnp.float32)
+    with scope("drain"):
+        for t in (1, 2, 3):
+            for c in range(pieces):
+                left_copy(t, c).wait_send()
+
+        @pl.when(target != core)
+        def _():
+            for c in range(pieces):
+                left_copy(0, c).wait_send()
+
+        right_copy.wait_send()
+
+        @pl.when(crossing)
+        def _():
+            for odd, (order, cut) in enumerate(cuts):
+
+                @pl.when(parity == odd)
+                def _():
+                    wait_sent(order[cut:])
+                    pl.when(jnp.logical_not(held_back))(functools.partial(wait_sent, order[:cut]))
+
+    def drain_level():
+        for j, n in by_plane:
+            if n < per_core:
+
+                @pl.when(is_near[j])
+                def _():
+                    near_copy(j, n).wait_send()
+
+            else:
+                near_copy(j, n).wait_send()
+
+    pl.when(jnp.logical_and(level, jnp.logical_not(held_back)))(drain_level)
     with scope("cross"):
         for c in range(per_core):
             cross_copy(0, c).wait_recv()
@@ -487,39 +549,7 @@
         scaled, scale = centre(mixed.astype(jnp.float32), mid_gain_ref[...])
         out_ref[...] = (dot(scaled, out_w_ref[...]) * (gate[...] * scale)).astype(jnp.bfloat16)
 
-    with scope("drain"):
-        for t in (1, 2, 3):
-            for c in range(pieces):
-                left_copy(t, c).wait_send()
-
-        @pl.when(target != core)
-        def _():
-            for c in range(pieces):
-                left_copy(0, c).wait_send()
-
-        right_copy.wait_send()
-
-        @pl.when(crossing)
-        def _():
-            for j, n in last_sends:
-                relay_copy(j, n).wait_send()
-
-            @pl.when(jnp.logical_not(held_back))
-            def _():
-                for j, n in first_sends:
-                    relay_copy(j, n).wait_send()
-
-        @pl.when(level)
-        def _():
-            for j, n in by_plane:
-                if n < per_core:
-
-                    @pl.when(is_near[j])
-                    def _():
-                        near_copy(j, n).wait_send()
-
-                else:
-                    near_copy(j, n).wait_send()
+    pl.when(jnp.logical_and(level, held_back))(drain_level)
 
 
 def triangle(planes, lines, pair_rows, in_gain, left_weight, right_weight, mid_gain, out_weight, out_gate):

time: 14 us -> 13.6 us (0.971)
  the two profiles are of different devices: /device:TPU:13 before, /device:TPU:17 now
where the time goes in v7:
time: 13.6 us; the launch traced here: 13.4 us
  Pallas kernels  12.8 us (94%)
  local copies, waits for them, and re-layouts  0.64 us (5%)
    pallas_call x1, Pallas kernels, triangle(): pl.pallas_call(functools.partial(triangle_kernel, rows, cols, planes, lin...  12.8 us
    unnamed x1, local copies, waits for them, and re-layouts  0.64 us

profile of v7, /device:TPU:17, one launch (start us, length us, event | category | flops | bytes accessed | tf_op | source)
XLA Modules:
  0.0 13.4 jit_solution(8931757627074073647)
XLA Ops:
  0.0 12.8 %shard_map.73 = bf16[288,128]{1,0:T(8,128)(2,1)S(1)} custom-call(bf16[12,24,128]{2,1,0:T(8,128)(2,1)} %refs_0_.1, f32[1,128]{1,0:T(1,128)} %bitcast.4, bf16[128,128]{1,0:T(8,128)(2,1)} %refs_2_.1, bf16[128,128]{1,0:T(8,128)(2,1)} %refs_3_.1, f32[1,128]{1,0:T(1,128)} %bitcast.5, bf16[128,128]{1,0:T(8,128)(2,1)} %refs_5_.1, bf16[128,128]{1,0:T(8,128)(2,1)} %refs_6_.1), custom_call_target="tpu_custom_call" | custom-call | tf_op jit(solution)/shard_map/pallas_call | solution.py:563
  12.8 0.6 %copy.9 = bf16[12,24,128]{2,1,0:T(8,128)(2,1)} copy(bf16[12,24,128]{2,1,0:T(8,128)(2,1)S(1)} %bitcast.3) | data formatting | bytes 147456

commit v8 on v7

--- a/solution.py
+++ b/solution.py
@@ -481,6 +481,39 @@
                             near_copy(j, n).start()
 
     count = rows * 2 * planes
+    with scope("drain"):
+        for t in (1, 2, 3):
+            for c in range(pieces):
+                left_copy(t, c).wait_send()
+
+        @pl.when(target != core)
+        def _():
+            for c in range(pieces):
+                left_copy(0, c).wait_send()
+
+        right_copy.wait_send()
+
+        @pl.when(crossing)
+        def _():
+            for odd, (order, cut) in enumerate(cuts):
+
+                @pl.when(parity == odd)
+                def _():
+                    wait_sent(order[cut:])
+                    pl.when(jnp.logical_not(held_back))(functools.partial(wait_sent, order[:cut]))
+
+    def drain_level():
+        for j, n in by_plane:
+            if n < per_core:
+
+                @pl.when(is_near[j])
+                def _():
+                    near_copy(j, n).wait_send()
+
+            else:
+                near_copy(j, n).wait_send()
+
+    pl.when(jnp.logical_and(level, jnp.logical_not(held_back)))(drain_level)
     for c in range(per_core):
         with scope(f"own{c}"):
 
@@ -493,39 +526,6 @@
     with scope("sum"):
         for c in range(per_core):
             part32[0, c] = inbox[own_at + c].astype(jnp.float32) + inbox[near_at + c].astype(jnp.float32)
-    with scope("drain"):
-        for t in (1, 2, 3):
-            for c in range(pieces):
-                left_copy(t, c).wait_send()
-
-        @pl.when(target != core)
-        def _():
-            for c in range(pieces):
-                left_copy(0, c).wait_send()
-
-        right_copy.wait_send()
-
-        @pl.when(crossing)
-        def _():
-            for odd, (order, cut) in enumerate(cuts):
-
-                @pl.when(parity == odd)
-                def _():
-                    wait_sent(order[cut:])
-                    pl.when(jnp.logical_not(held_back))(functools.partial(wait_sent, order[:cut]))
-
-    def drain_level():
-        for j, n in by_plane:
-            if n < per_core:
-
-                @pl.when(is_near[j])
-                def _():
-                    near_copy(j, n).wait_send()
-
-            else:
-                near_copy(j, n).wait_send()
-
-    pl.when(jnp.logical_and(level, jnp.logical_not(held_back)))(drain_level)
     with scope("cross"):
         for c in range(per_core):
             cross_copy(0, c).wait_recv()

time: 13.6 us -> 13.5 us (level)
  the two profiles are of different devices: /device:TPU:17 before, /device:TPU:13 now
where the time goes in v8:
time: 13.5 us; the launch traced here: 13.3 us
  Pallas kernels  12.7 us (94%)
  local copies, waits for them, and re-layouts  0.64 us (5%)
    pallas_call x1, Pallas kernels, triangle(): pl.pallas_call(functools.partial(triangle_kernel, rows, cols, planes, lin...  12.7 us
    unnamed x1, local copies, waits for them, and re-layouts  0.64 us

profile of v8, /device:TPU:13, one launch (start us, length us, event | category | flops | bytes accessed | tf_op | source)
XLA Modules:
  0.0 13.3 jit_solution(6705402326872608393)
XLA Ops:
  0.0 12.7 %shard_map.73 = bf16[288,128]{1,0:T(8,128)(2,1)S(1)} custom-call(bf16[12,24,128]{2,1,0:T(8,128)(2,1)} %refs_0_.1, f32[1,128]{1,0:T(1,128)} %bitcast.4, bf16[128,128]{1,0:T(8,128)(2,1)} %refs_2_.1, bf16[128,128]{1,0:T(8,128)(2,1)} %refs_3_.1, f32[1,128]{1,0:T(1,128)} %bitcast.5, bf16[128,128]{1,0:T(8,128)(2,1)} %refs_5_.1, bf16[128,128]{1,0:T(8,128)(2,1)} %refs_6_.1), custom_call_target="tpu_custom_call" | custom-call | tf_op jit(solution)/shard_map/pallas_call | solution.py:563
  12.7 0.6 %copy.9 = bf16[12,24,128]{2,1,0:T(8,128)(2,1)} copy(bf16[12,24,128]{2,1,0:T(8,128)(2,1)S(1)} %bitcast.3) | data formatting | bytes 147456

commit v9 on v8

--- a/solution.py
+++ b/solution.py
@@ -416,9 +416,21 @@
         def _():
             pl.semaphore_wait(near_sem, 1)
 
+    def near_after_go():
+        pl.semaphore_wait(go_sem, 1)
+        for n in range(chunks):
+            near_copy(0, n).start()
+
     for j in range(2):
         for c in range(pieces):
             block(j, c)
+        if j == 0:
+            with scope("held0"):
+
+                @pl.when(jnp.logical_and(level, jnp.logical_and(held_back, is_near[0])))
+                def _():
+                    pl.when(jnp.logical_not(from_own))(near_after_go)
+
 
     by_plane = [(j, n) for j in range(2) for n in range(chunks)]
     by_need = sorted(by_plane, key=lambda at: waits(*at))
@@ -470,15 +482,15 @@
                     pl.when(parity == odd)(functools.partial(wait_sent, order[:cut]))
                 pl.semaphore_signal(go_sem, inc=1, device_id=device(z, 0, second), device_id_type=MESH)
 
-            @pl.when(level)
+            @pl.when(jnp.logical_and(level, is_near[0]))
+            def _():
+                pl.when(from_own)(near_after_go)
+
+            @pl.when(jnp.logical_and(level, is_near[1]))
             def _():
                 pl.semaphore_wait(go_sem, 1)
-                for j in range(2):
-
-                    @pl.when(is_near[j])
-                    def _():
-                        for n in range(chunks):
-                            near_copy(j, n).start()
+                for n in range(chunks):
+                    near_copy(1, n).start()
 
     count = rows * 2 * planes
     with scope("drain"):

time: 13.5 us -> 13.5 us (level)
  no operation moved by 1% of the time
where the time goes in v9:
time: 13.5 us; the launch traced here: 13.3 us
  Pallas kernels  12.7 us (94%)
  local copies, waits for them, and re-layouts  0.64 us (5%)
    pallas_call x1, Pallas kernels, triangle(): pl.pallas_call(functools.partial(triangle_kernel, rows, cols, planes, lin...  12.7 us
    unnamed x1, local copies, waits for them, and re-layouts  0.64 us

profile of v9, /device:TPU:13, one launch (start us, length us, event | category | flops | bytes accessed | tf_op | source)
XLA Modules:
  0.0 13.3 jit_solution(5152322572539394518)
XLA Ops:
  0.0 12.7 %shard_map.73 = bf16[288,128]{1,0:T(8,128)(2,1)S(1)} custom-call(bf16[12,24,128]{2,1,0:T(8,128)(2,1)} %refs_0_.1, f32[1,128]{1,0:T(1,128)} %bitcast.4, bf16[128,128]{1,0:T(8,128)(2,1)} %refs_2_.1, bf16[128,128]{1,0:T(8,128)(2,1)} %refs_3_.1, f32[1,128]{1,0:T(1,128)} %bitcast.5, bf16[128,128]{1,0:T(8,128)(2,1)} %refs_5_.1, bf16[128,128]{1,0:T(8,128)(2,1)} %refs_6_.1), custom_call_target="tpu_custom_call" | custom-call | tf_op jit(solution)/shard_map/pallas_call | solution.py:575
  12.7 0.6 %copy.9 = bf16[12,24,128]{2,1,0:T(8,128)(2,1)} copy(bf16[12,24,128]{2,1,0:T(8,128)(2,1)S(1)} %bitcast.3) | data formatting | bytes 147456

commit v10 on v9

--- a/solution.py
+++ b/solution.py
@@ -466,7 +466,7 @@
             pl.when(parity == 0)(lambda: relay_all(by_plane))
             pl.when(parity == 1)(lambda: relay_all(by_need))
 
-    cuts = (by_plane, 2 * chunks - chunks // 4), (by_need, 2 * chunks - per_core)
+    cuts = (by_plane, 2 * chunks - chunks // 4), (by_need, 2 * chunks - per_core - 3)
 
     def wait_sent(order):
         for j, n in order:

time: 13.5 us -> 13.5 us (level)
  no operation moved by 1% of the time
where the time goes in v10:
time: 13.5 us; the launch traced here: 13.3 us
  Pallas kernels  12.7 us (94%)
  local copies, waits for them, and re-layouts  0.64 us (5%)
    pallas_call x1, Pallas kernels, triangle(): pl.pallas_call(functools.partial(triangle_kernel, rows, cols, planes, lin...  12.7 us
    unnamed x1, local copies, waits for them, and re-layouts  0.64 us

profile of v10, /device:TPU:13, one launch (start us, length us, event | category | flops | bytes accessed | tf_op | source)
XLA Modules:
  0.0 13.3 jit_solution(10312632881739970439)
XLA Ops:
  0.0 12.7 %shard_map.73 = bf16[288,128]{1,0:T(8,128)(2,1)S(1)} custom-call(bf16[12,24,128]{2,1,0:T(8,128)(2,1)} %refs_0_.1, f32[1,128]{1,0:T(1,128)} %bitcast.4, bf16[128,128]{1,0:T(8,128)(2,1)} %refs_2_.1, bf16[128,128]{1,0:T(8,128)(2,1)} %refs_3_.1, f32[1,128]{1,0:T(1,128)} %bitcast.5, bf16[128,128]{1,0:T(8,128)(2,1)} %refs_5_.1, bf16[128,128]{1,0:T(8,128)(2,1)} %refs_6_.1), custom_call_target="tpu_custom_call" | custom-call | tf_op jit(solution)/shard_map/pallas_call | solution.py:575
  12.7 0.6 %copy.9 = bf16[12,24,128]{2,1,0:T(8,128)(2,1)} copy(bf16[12,24,128]{2,1,0:T(8,128)(2,1)S(1)} %bitcast.3) | data formatting | bytes 147456
